TPU v7x, 256 devices: a whole 4x4x8 slice. The times are simulated.
256 devices in a mesh: tm: 2 (over y_lo), row: 16 (over y_hi, z), col: 8 (over x, core).
Axes of the slice: x: 4, y: 4 (y_hi: 2, y_lo: 2; y = y_hi * 2 + y_lo), z: 8, core: 2. Of those that a mesh axis runs over, the one named last changes fastest.
Arguments:
- returns: bfloat16 [272, 16384], P('tm', ('row', 'col')), may hold values from -60 to 60
- window: int32 [1], replicated, may hold values from 200 to 256
- out_days: int32 [4], replicated, may hold values from 255 to 271
Outputs:
- correlation: bfloat16 [4, 16384, 16384], P(None, 'row', ('col', 'tm'))
Inputs may be any that keep to these rules, and one draw needn't show every extreme that they name: One window length for all days. `out_days`: days may repeat.
All inputs are finite; a program needn't handle non-finite values.
Results may differ from a plain program's by a relative error of at most 0.001.
Values may be sent and summed in bfloat16 or wider, within the bound.
No kernel may reach another device: no remote copies, remote signals or barrier semaphores. Data moves between devices by JAX's collectives and lax.ppermute only.
A program may use at most 128 MiB of HBM per device.

v0:
```python
import jax
import jax.numpy as jnp
from jax import lax
from jax.sharding import PartitionSpec as P


def moments(mask, block):
    series = block.astype(jnp.float32)
    first = jnp.dot(mask, series, precision=lax.Precision.HIGHEST)
    second = jnp.dot(mask, series * series, precision=lax.Precision.HIGHEST)
    return (first, second)


def on_device(returns, window, out_days):
    width = window[0]
    wide = width.astype(jnp.float32)
    tm_count = lax.axis_size("tm")
    tm_index = lax.axis_index("tm")
    share = lax.axis_size("row") // lax.axis_size("col")
    local = lax.all_gather(returns, "tm", axis=0, tiled=True)
    row_series = lax.all_gather(local, "col", axis=1, tiled=True)
    block_width = row_series.shape[1]
    col_index = lax.axis_index("col")
    range_width = share * block_width
    half = range_width // tm_count
    half_start = tm_index * half
    range_start = col_index * range_width
    wanted_start = range_start + half_start
    everything = lax.all_gather(row_series, "row", axis=1, tiled=True)
    col_series = lax.dynamic_slice_in_dim(everything, wanted_start, half, 1)
    day_count = local.shape[0]
    day_ids = jnp.arange(day_count, dtype=jnp.int32)
    inside = (day_ids[None, :] <= out_days[:, None]) & (
        day_ids[None, :] > out_days[:, None] - width
    )
    mask = jnp.where(inside, 1.0, 0.0).astype(jnp.float32)
    weighted = mask.astype(jnp.bfloat16)[:, :, None] * row_series[None, :, :]
    gram = jnp.einsum("kda,db->kab", weighted, col_series, preferred_element_type=jnp.float32)
    first_rows, second_rows = moments(mask, row_series)
    first_cols, second_cols = moments(mask, col_series)
    scale_rows = lax.rsqrt((second_rows - first_rows * first_rows / wide) / wide + 1e-06)
    scale_cols = lax.rsqrt((second_cols - first_cols * first_cols / wide) / wide + 1e-06)
    cov = gram - first_rows[:, :, None] * first_cols[:, None, :] / wide
    return (cov * scale_rows[:, :, None] * scale_cols[:, None, :] / wide).astype(jnp.bfloat16)


def solution(mesh):
    return jax.shard_map(
        on_device,
        mesh=mesh,
        in_specs=(P("tm", ("row", "col")), P(), P()),
        out_specs=P(None, "row", ("col", "tm")),
        check_vma=False,
    )
```

profile of v0, /device:TPU:36, one launch (start us, length us, event | category | flops | bytes accessed | tf_op | source)
XLA Modules:
  0.0 185.7 jit_solution(15276482759653825243)
XLA Ops:
  6.5 0.0 all-gather.2.cloned.1.call-start
  6.5 4.8 %all_gather.9 = bf16[272,128]{1,0:T(8,128)(2,1)S(1)} all-gather(bf16[136,128]{1,0:T(8,128)(2,1)} %param.3), channel_id=1, replica_groups=mesh['tm'=2,'row'=16,'col'=8] {'tm'}, dimensions={0}, use_global_device_ids=true | all-gather | bytes 104448 | tf_op jit(solution)/shard_map/all_gather | solution.py:20
  11.3 13.0 %all_gather.10 = bf16[272,1024]{1,0:T(8,128)(2,1)} all-gather(bf16[272,128]{1,0:T(8,128)(2,1)S(1)} %all_gather.9), channel_id=1, replica_groups=mesh['tm'=2,'row'=16,'col'=8] {'col'}, dimensions={1}, use_global_device_ids=true | all-gather | bytes 626688 | tf_op jit(solution)/shard_map/all_gather | solution.py:21
  24.3 0.0 all-gather.2.cloned.1.call-update
  25.0 0.7 broadcast_subtract_fusion
  25.6 0.7 select_convert_fusion
  26.4 1.4 fusion.41
  27.8 1.8 fusion.18
  29.6 136.0 %all-gather.2.cloned.1.call-done = bf16[272,16384]{1,0:T(8,128)(2,1)} async-done(((bf16[272,1024]{1,0:T(8,128)(2,1)}), bf16[272,16384]{1,0:T(8,128)(2,1)}) %all-gather.2.cloned.1.call-update) | async-done | bytes 8912912 | tf_op jit(solution)/shard_map/all_gather | solution.py:29
  165.7 1.4 fusion.35
  167.1 1.8 fusion.30
  169.0 9.9 %divide_convert_fusion = bf16[4,1024,1024]{2,1,0:T(8,128)(2,1)} fusion(f32[4,1024]{1,0:T(4,128)S(1)} %fusion.30, f32[4,1024]{1,0:T(4,128)S(1)} %fusion.18, f32[]{:T(128)S(6)} %convert_element_type.20, f32[4,1024]{1,0:T(4,128)S(1)} %fusion.35, f32[4,1024]{1,0:T(4,128)S(1)} %fusion.41, bf16[272,1024]{1,0:T(8,128)(2,1)} %all_gather.10, ...), kind=kOutput, calls=%fused_computation | convolution fusion | flops 2312175616 | bytes 9570440 | tf_op jit(solution)/shard_map/kda,db->kab/dot_general | solution.py:38
Async XLA Ops:
  6.5 159.2 %all-gather.2.cloned.1.call-start = ((), (), s32[]{:S(2)}) async-start(), calls=%async_computation | async-start | bytes 9469952 | tf_op jit(solution)/shard_map/all_gather | solution.py:29
Sparse Core Ops, SparseCore 0:
  24.4 141.2 all-gather.1
where the time goes:
time: 188 us; the launch traced here: 186 us
  waiting for transfers between devices  136 us (72%)
  blocking collectives  17.8 us (9%)
  matrix products  16.4 us (9%)
  between operations  14.1 us (8%)
    all_gather x1, waiting for transfers between devices, on_device(): everything = lax.all_gather(row_series, 'row', axis=1, tiled=True)  136 us
    all_gather x1, blocking collectives, on_device(): row_series = lax.all_gather(local, 'col', axis=1, tiled=True)  13 us
    dot_general x1, matrix products, on_device(): jnp.einsum('kda,db->kab', weighted, col_series, preferred_element_type=jn...  9.9 us
    all_gather x1, blocking collectives, on_device(): local = lax.all_gather(returns, 'tm', axis=0, tiled=True)  4.8 us
  transfers between devices with their start and end apart: 1, of which 1 were waited for; matrix products, arithmetic and copies ran while one was open for 3% of the time, Pallas kernels for 0%

commit v1 on v0

v1 whole, which is shorter than its diff:
```python
import functools
import itertools

import jax
import jax.numpy as jnp
from jax import lax
from jax.experimental import pallas as pl
from jax.experimental.pallas import tpu as pltpu
from jax.sharding import Mesh
from jax.sharding import PartitionSpec as P

AXES = ("yl", "yh", "zh", "zq", "x", "c")
SIZES = (2, 2, 2, 4, 4, 2)
LANES = 128


def place(yl, yh, zh, zq, x, c):
    number = 0
    for size, index in zip(SIZES, (yl, yh, zh, zq, x, c)):
        number = number * size + index
    return number


def corner_turn():
    pairs = []
    for yl, yh, zh, zq, x, c in itertools.product(*map(range, SIZES)):
        to_x, to_c, to_yl = 2 * yh + zh, zq // 2, zq % 2
        to_yh = yh if yl == to_yl else 1 - yh
        to = (to_yl, to_yh, c, (zq + x - to_x) % 4, to_x, to_c)
        pairs.append((place(yl, yh, zh, zq, x, c), place(*to)))
    return pairs


def ring(size, step):
    return [(i, (i + step) % size) for i in range(size)]


def two_apart(size):
    return [(i, (i + 2 - 4 * (i % 2)) % size) for i in range(size)]


def days_by_assets(block):
    columns = [
        jnp.concatenate([block[h, c].astype(jnp.float32) for h in range(2)], axis=0) for c in range(2)
    ]
    return jnp.concatenate(columns, axis=1)


def statistics(series, facts, k):
    width, last = facts[0], facts[1 + k]
    wide = width.astype(jnp.float32)
    day = lax.broadcasted_iota(jnp.int32, series.shape, 0)
    kept = jnp.where((day <= last) & (day > last - width), series, 0.0)
    first = jnp.sum(kept, axis=0, keepdims=True)
    second = jnp.sum(kept * kept, axis=0, keepdims=True)
    scale = lax.rsqrt((second - first * first / wide) / wide + 1e-06)
    return first, scale, wide


def prepare_rows(facts, own, before, after, across, left, stats):
    x = lax.axis_index("x")
    for ref, step in ((own, 0), (before, 3), (after, 1), (across, 2)):
        quarter = lax.rem(x + step, 4)
        rows = pl.ds(pl.multiple_of(quarter * 256, 256), 256)
        series = days_by_assets(ref)
        days, assets = series.shape
        spare = days - 256
        main = series[:256].T
        folded = jnp.concatenate([series[256:], jnp.zeros((LANES - spare, assets), jnp.float32)], axis=0).T
        columns = []
        for k in range(4):
            first, scale, _ = statistics(series, facts, k)
            columns.append((first, scale))
            width, last = facts[0], facts[1 + k]
            slot = lax.broadcasted_iota(jnp.int32, (assets, LANES), 1)
            low = jnp.where(slot > last - width, main[:, :LANES], 0.0)
            low = jnp.where((slot < spare) & (slot + 256 <= last), folded, low)
            left[k, rows, :LANES] = low.astype(jnp.bfloat16)
            left[k, rows, LANES:] = jnp.where(
                slot + LANES > last - width, main[:, LANES:], 0.0
            ).astype(jnp.bfloat16)
        table = [first for first, _ in columns] + [scale for _, scale in columns]
        table.append(jnp.zeros((LANES - 8, assets), jnp.float32))
        stats[rows, :] = jnp.concatenate(table, axis=0).T


def quarter_of_columns(step, facts, left, stats, block, *rest):
    out, result, sems = rest[-3:]
    turn = lax.axis_index("x") + lax.axis_index("zq") - 2 * lax.axis_index("c") - lax.axis_index("yl")
    quarter = lax.rem(turn + step + 8, 4)
    columns = pl.ds(pl.multiple_of(quarter * 256, 256), 256)
    series = days_by_assets(block)
    spare = series.shape[0] - 256
    common = series[spare:256].astype(jnp.bfloat16)
    copies = []
    for k in range(4):
        first, scale, wide = statistics(series, facts, k)
        mean, scale = first / wide, scale / wide
        slot = lax.broadcasted_iota(jnp.int32, (spare, series.shape[1]), 0)
        head = jnp.where(slot + 256 <= facts[1 + k], series[256:], series[:spare])
        right = jnp.concatenate([head.astype(jnp.bfloat16), common], axis=0)
        for i in range(4):
            rows = slice(i * 256, (i + 1) * 256)
            gram = jnp.dot(left[k, rows, :], right, preferred_element_type=jnp.float32)
            cov = gram - stats[rows, k : k + 1] * mean
            result[k, rows, :] = (cov * stats[rows, 4 + k : 5 + k] * scale).astype(jnp.bfloat16)
        copy = pltpu.make_async_copy(result.at[k], out.at[k, :, columns], sems.at[k])
        copy.start()
        copies.append(copy)
    for copy in copies:
        copy.wait()


def on_device(returns, window, out_days):
    facts = jnp.concatenate([window, out_days])
    pair = lax.all_gather(returns, "c", axis=0)
    turned = lax.ppermute(pair, AXES, corner_turn())
    own_rows = lax.all_gather(pair, "yl", axis=0)
    rows = [own_rows]
    for links in (ring(4, 1), ring(4, 3), ring(4, 2)):
        rows.append(lax.ppermute(own_rows, "x", links))
    other = lax.ppermute(turned, "yh", ring(2, 1))
    half = lax.axis_index("yl") + lax.axis_index("yh") + lax.axis_index("x") // 2
    own_columns = jnp.where(half % 2 == 0, jnp.stack([turned, other]), jnp.stack([other, turned]))
    columns = [(0, own_columns)]
    for step, links in ((3, ring(8, 1)), (1, ring(8, 7)), (2, two_apart(8))):
        columns.append((step, lax.ppermute(own_columns, ("zh", "zq"), links)))

    smem, vmem = pl.BlockSpec(memory_space=pltpu.SMEM), pl.BlockSpec(memory_space=pltpu.VMEM)
    anywhere = pl.BlockSpec(memory_space=pl.ANY)
    assets = 1024
    left, stats = pl.pallas_call(
        prepare_rows,
        out_shape=(
            jax.ShapeDtypeStruct((4, assets, 256), jnp.bfloat16),
            jax.ShapeDtypeStruct((assets, LANES), jnp.float32),
        ),
        in_specs=[smem] + [vmem] * 4,
        out_specs=(vmem, vmem),
        cost_estimate=pl.CostEstimate(flops=2_000_000_000, bytes_accessed=4_000_000, transcendentals=0),
        name="prepare_rows",
    )(facts, *rows)
    out = None
    for step, block in columns:
        out = pl.pallas_call(
            functools.partial(quarter_of_columns, step),
            out_shape=jax.ShapeDtypeStruct((4, assets, assets), jnp.bfloat16),
            in_specs=[smem, vmem, vmem, vmem] + ([anywhere] if out is not None else []),
            out_specs=anywhere,
            scratch_shapes=[pltpu.VMEM((4, assets, 256), jnp.bfloat16), pltpu.SemaphoreType.DMA((4,))],
            input_output_aliases={} if out is None else {4: 0},
            cost_estimate=pl.CostEstimate(flops=2_000_000_000, bytes_accessed=4_000_000, transcendentals=0),
            name="quarter",
        )(*([facts, left, stats, block] + ([out] if out is not None else [])))
    return out


def solution(mesh):
    fine = Mesh(mesh.devices.reshape(SIZES), AXES)
    return jax.shard_map(
        on_device,
        mesh=fine,
        in_specs=(P("yl", ("yh", "zh", "zq", "x", "c")), P(), P()),
        out_specs=P(None, ("yh", "zh", "zq"), ("x", "c", "yl")),
        check_vma=False,
    )
```

time: 188 us -> 55 us (0.29); the launches traced: 186 us -> 54.7 us
  waiting for transfers between devices: 136 us -> 0.99 us
  starting transfers between devices: 0.01 us -> 20.7 us
  Pallas kernels: 0 us -> 20.5 us
  matrix products: 16.4 us -> 0 us
  between operations: 14.1 us -> 0.95 us
  blocking collectives: 17.8 us -> 7.03 us
  local copies, waits for them, and re-layouts: 0 us -> 3.23 us
    all_gather x1 -> x0, waiting for transfers between devices: 136 us -> none  [on_device(): everything = lax.all_gather(row_series, 'row', axis=1, tiled=True)]
    ppermute x0 -> x8, starting transfers between devices: none -> 20.7 us  [the longest x1 7.56 us: on_device(): turned = lax.ppermute(pair, AXES, corner_turn())]
    pallas_call x0 -> x5, Pallas kernels: none -> 20.5 us  [the longest x4 16.4 us: on_device(): pl.pallas_call(functools.partial(quarter_of_columns, step), out_shape=jax...]
    dot_general x5 -> x0, matrix products: 16.4 us -> none  [the longest x1 9.9 us: on_device(): jnp.einsum('kda,db->kab', weighted, col_series, preferred_element_type=jn...]
    all_gather x2, blocking collectives: 17.8 us -> 7.03 us  [the longest x1 4.98 us: on_device(): own_rows = lax.all_gather(pair, 'yl', axis=0)]
    unnamed x0 -> x16, local copies, waits for them, and re-layouts: none -> 3.23 us
  transfers between devices with their start and end apart: 1 -> 8, of which waited for: 1 -> 1; matrix products, arithmetic and copies ran while one was open for 3% -> 2% of each run, Pallas kernels for 0% -> 30%
where the time goes in v1:
time: 55 us; the launch traced here: 54.7 us
  starting transfers between devices  20.7 us (38%)
  Pallas kernels  20.5 us (37%)
  blocking collectives  7.03 us (13%)
  local copies, waits for them, and re-layouts  3.23 us (6%)
  other arithmetic  1.33 us (2%)
  waiting for transfers between devices  0.99 us (2%)
  between operations  0.95 us (2%)
    pallas_call x4, Pallas kernels, on_device(): pl.pallas_call(functools.partial(quarter_of_columns, step), out_shape=jax...  16.4 us
    ppermute x1, starting transfers between devices, on_device(): turned = lax.ppermute(pair, AXES, corner_turn())  7.56 us
    ppermute x3, starting transfers between devices, on_device(): columns.append((step, lax.ppermute(own_columns, ('zh', 'zq'), links)))  6.12 us
    all_gather x1, blocking collectives, on_device(): own_rows = lax.all_gather(pair, 'yl', axis=0)  4.98 us
    ppermute x1, starting transfers between devices, on_device(): other = lax.ppermute(turned, 'yh', ring(2, 1))  4.95 us
    pallas_call x1, Pallas kernels, on_device(): pl.pallas_call(prepare_rows, out_shape=(jax.ShapeDtypeStruct((4, assets,...  4.05 us
    unnamed x16, local copies, waits for them, and re-layouts  3.23 us
    all_gather x1, blocking collectives, on_device(): pair = lax.all_gather(returns, 'c', axis=0)  2.05 us
  transfers between devices with their start and end apart: 8, of which 1 were waited for; matrix products, arithmetic and copies ran while one was open for 2% of the time, Pallas kernels for 30%

profile of v1, /device:TPU:36, one launch (start us, length us, event | category | flops | bytes accessed | tf_op | source)
XLA Modules:
  0.0 54.7 jit_solution(3578323400201825117)
XLA Ops:
  0.0 2.1 %all-gather = bf16[272,128]{1,0:T(8,128)(2,1)S(1)} all-gather(bf16[136,128]{1,0:T(8,128)(2,1)} %param.3), channel_id=2, replica_groups=mesh['yl'=2,'yh'=2,'zh'=2,'zq'=4,'x'=4,'c'=2] {'c'}, dimensions={0}, use_global_device_ids=true | all-gather | bytes 104448 | tf_op jit(solution)/shard_map/all_gather | solution.py:116
  2.1 7.6 %collective-permute-start.3 = (bf16[2,136,128]{2,1,0:T(8,128)(2,1)S(1)}, bf16[2,136,128]{2,1,0:T(8,128)(2,1)S(1)}, u32[]{:S(2)}, u32[]{:S(2)}) collective-permute-start(bf16[2,136,128]{2,1,0:T(8,128)(2,1)S(1)} %bitcast.4), channel_id=1, source_target_pairs={{0,0},{1,32},{2,8},{3,40},{4,16},{5,48},{6,24},{7,56},{8,200},{9,2... | collective-permute-start | bytes 208904 | tf_op jit(solution)/shard_map/ppermute | solution.py:117
  9.6 5.0 %all-gather.1 = bf16[4,136,128]{2,1,0:T(8,128)(2,1)S(1)} all-gather(bf16[2,136,128]{2,1,0:T(8,128)(2,1)S(1)} %bitcast.5), channel_id=3, replica_groups=mesh['yl'=2,'yh'=2,'zh'=2,'zq'=4,'x'=4,'c'=2] {'yl'}, dimensions={0}, use_global_device_ids=true | all-gather | bytes 208896 | tf_op jit(solution)/shard_map/all_gather | solution.py:118
  14.6 2.0 %collective-permute-start.1 = (bf16[2,2,136,128]{3,2,1,0:T(8,128)(2,1)S(1)}, bf16[2,2,136,128]{3,2,1,0:T(8,128)(2,1)S(1)}, u32[]{:S(2)}, u32[]{:S(2)}) collective-permute-start(bf16[2,2,136,128]{3,2,1,0:T(8,128)(2,1)S(1)} %bitcast.7), channel_id=1, source_target_pairs={{0,6},{2,0},{4,2},{6,4},{1,7},{3,1},{5,3},{7,5},{8,14},{10,8},{12,... | collective-permute-start | bytes 417800 | tf_op jit(solution)/shard_map/ppermute | solution.py:121
  16.6 0.0 collective-permute-start.2
  17.3 4.9 %collective-permute-start.4 = (bf16[2,136,128]{2,1,0:T(8,128)(2,1)S(1)}, bf16[2,136,128]{2,1,0:T(8,128)(2,1)S(1)}, u32[]{:S(2)}, u32[]{:S(2)}) collective-permute-start(bf16[2,136,128]{2,1,0:T(8,128)(2,1)S(1)} %collective-permute-done.3), channel_id=1, source_target_pairs={{0,64},{64,0},{1,65},{65,1},{2,66},{66,2},{3,67},{67,3},{4,68},{68... | collective-permute-start | bytes 208904 | tf_op jit(solution)/shard_map/ppermute | solution.py:122
  22.2 1.3 %pad_add_fusion.facts = s32[5]{0:T(128)} fusion(s32[4]{0:T(128)} %param.5, s32[1]{0:T(128)S(6)} %copy.10), kind=kLoop, calls=%fused_computation.1 | loop fusion | flops 5 | bytes 40 | tf_op jit(solution)/shard_map/concatenate | solution.py:115
  23.6 1.0 %collective-permute-done.4 = bf16[2,136,128]{2,1,0:T(8,128)(2,1)S(1)} collective-permute-done((bf16[2,136,128]{2,1,0:T(8,128)(2,1)S(1)}, bf16[2,136,128]{2,1,0:T(8,128)(2,1)S(1)}, u32[]{:S(2)}, u32[]{:S(2)}) %collective-permute-start.4) | collective-permute-done | bytes 69664 | tf_op jit(solution)/shard_map/ppermute | solution.py:122
  24.6 0.1 collective-permute-start.7
  24.7 2.0 %collective-permute-start.6 = (bf16[2,2,136,128]{3,2,1,0:T(8,128)(2,1)S(1)}, bf16[2,2,136,128]{3,2,1,0:T(8,128)(2,1)S(1)}, u32[]{:S(2)}, u32[]{:S(2)}) collective-permute-start(bf16[2,2,136,128]{3,2,1,0:T(8,128)(2,1)S(1)} %maximum_select_fusion.block), channel_id=1, source_target_pairs={{0,56},{8,0},{16,8},{24,16},{32,24},{40,32},{48,40},{56,48},{1,57}... | collective-permute-start | bytes 417800 | tf_op jit(solution)/shard_map/ppermute | solution.py:127
  26.7 0.0 collective-permute-done.before
  26.7 4.0 %collective-permute-start.5 = (bf16[2,2,136,128]{3,2,1,0:T(8,128)(2,1)S(1)}, bf16[2,2,136,128]{3,2,1,0:T(8,128)(2,1)S(1)}, u32[]{:S(2)}, u32[]{:S(2)}) collective-permute-start(bf16[2,2,136,128]{3,2,1,0:T(8,128)(2,1)S(1)} %maximum_select_fusion.block), channel_id=1, source_target_pairs={{0,16},{8,56},{16,32},{24,8},{32,48},{40,24},{48,0},{56,40},{1,17}... | collective-permute-start | bytes 417800 | tf_op jit(solution)/shard_map/ppermute | solution.py:127
  30.7 0.0 collective-permute-done.1.after
  30.7 0.6 %copy-done.6 = bf16[2,2,136,128]{3,2,1,0:T(8,128)(2,1)} copy-done((bf16[2,2,136,128]{3,2,1,0:T(8,128)(2,1)}, bf16[2,2,136,128]{3,2,1,0:T(8,128)(2,1)S(1)}, u32[]{:S(2)}) %copy-start.6) | copy-done | bytes 139288
  31.4 0.6 %copy-done.7 = bf16[2,2,136,128]{3,2,1,0:T(8,128)(2,1)} copy-done((bf16[2,2,136,128]{3,2,1,0:T(8,128)(2,1)}, bf16[2,2,136,128]{3,2,1,0:T(8,128)(2,1)S(1)}, u32[]{:S(2)}) %copy-start.7) | copy-done | bytes 139288
  32.0 4.1 %prepare_rows.1 = (bf16[4,1024,256]{2,1,0:T(8,128)(2,1)}, f32[1024,128]{1,0:T(8,128)}) custom-call(s32[5]{0:T(128)} %pad_add_fusion.facts, bf16[2,2,136,128]{3,2,1,0:T(8,128)(2,1)} %bitcast.9, bf16[2,2,136,128]{3,2,1,0:T(8,128)(2,1)} %copy-done.5, bf16[2,2,136,128]{3,2,1,0:T(8,128)(2,1)} %copy-done.6, bf16[2,2,136,128]{3,2,1,0:T(8,128)(2,1)} %copy-done.7), custom_call_target="tpu_custom_call" | custom-call | flops 2000000000 | bytes 4000000 | tf_op jit(solution)/shard_map/prepare_rows/pallas_call | solution.py:132
  36.1 4.1 %quarter.4.rest_0_ = bf16[4,1024,1024]{2,1,0:T(8,128)(2,1)} custom-call(s32[5]{0:T(128)} %pad_add_fusion.facts, bf16[4,1024,256]{2,1,0:T(8,128)(2,1)} %get-tuple-element.7.left, f32[1024,128]{1,0:T(8,128)} %get-tuple-element.8.stats, bf16[2,2,136,128]{3,2,1,0:T(8,128)(2,1)} %copy-done), custom_call_target="tpu_custom_call" | custom-call | flops 2000000000 | bytes 4000000 | tf_op jit(solution)/shard_map/quarter/pallas_call | solution.py:145
  40.2 0.0 collective-permute-done.7.block
  40.2 0.6 %copy-done.4 = bf16[2,2,136,128]{3,2,1,0:T(8,128)(2,1)} copy-done((bf16[2,2,136,128]{3,2,1,0:T(8,128)(2,1)}, bf16[2,2,136,128]{3,2,1,0:T(8,128)(2,1)S(1)}, u32[]{:S(2)}) %copy-start.4) | copy-done | bytes 139288
  40.8 4.1 %quarter.5.rest_0_ = bf16[4,1024,1024]{2,1,0:T(8,128)(2,1)} custom-call(s32[5]{0:T(128)} %pad_add_fusion.facts, bf16[4,1024,256]{2,1,0:T(8,128)(2,1)} %get-tuple-element.7.left, f32[1024,128]{1,0:T(8,128)} %get-tuple-element.8.stats, bf16[2,2,136,128]{3,2,1,0:T(8,128)(2,1)} %copy-done.4, ...), custom_call_target="tpu_custom_call", output_to_operand_aliasing={{}: (4, {})} | custom-call | flops 2000000000 | bytes 4000000 | tf_op jit(solution)/shard_map/quarter/pallas_call | solution.py:145
  45.0 0.6 %copy-done.3 = bf16[2,2,136,128]{3,2,1,0:T(8,128)(2,1)} copy-done((bf16[2,2,136,128]{3,2,1,0:T(8,128)(2,1)}, bf16[2,2,136,128]{3,2,1,0:T(8,128)(2,1)S(1)}, u32[]{:S(2)}) %copy-start.3) | copy-done | bytes 139288
  45.6 4.1 %quarter.6.rest_0_ = bf16[4,1024,1024]{2,1,0:T(8,128)(2,1)} custom-call(s32[5]{0:T(128)} %pad_add_fusion.facts, bf16[4,1024,256]{2,1,0:T(8,128)(2,1)} %get-tuple-element.7.left, f32[1024,128]{1,0:T(8,128)} %get-tuple-element.8.stats, bf16[2,2,136,128]{3,2,1,0:T(8,128)(2,1)} %copy-done.3, ...), custom_call_target="tpu_custom_call", output_to_operand_aliasing={{}: (4, {})} | custom-call | flops 2000000000 | bytes 4000000 | tf_op jit(solution)/shard_map/quarter/pallas_call | solution.py:145
  49.8 0.6 %copy-done.2 = bf16[2,2,136,128]{3,2,1,0:T(8,128)(2,1)} copy-done((bf16[2,2,136,128]{3,2,1,0:T(8,128)(2,1)}, bf16[2,2,136,128]{3,2,1,0:T(8,128)(2,1)S(1)}, u32[]{:S(2)}) %copy-start.2) | copy-done | bytes 139288
  50.4 4.1 %quarter.7 = bf16[4,1024,1024]{2,1,0:T(8,128)(2,1)} custom-call(s32[5]{0:T(128)} %pad_add_fusion.facts, bf16[4,1024,256]{2,1,0:T(8,128)(2,1)} %get-tuple-element.7.left, f32[1024,128]{1,0:T(8,128)} %get-tuple-element.8.stats, bf16[2,2,136,128]{3,2,1,0:T(8,128)(2,1)} %copy-done.2, bf16[4,1024,1024]{2,1,0:T(8,128)(2,1)} %quarter.6.rest_0_), custom_call_target="tpu_custom_call", output_to_operand_aliasing={{}: (4, {})} | custom-call | flops 2000000000 | bytes 4000000 | tf_op jit(solution)/shard_map/quarter/pallas_call | solution.py:145
  (17 shorter events, 0.0 us)
Async XLA Ops:
  2.1 15.2 %collective-permute-start.3 = (bf16[2,136,128]{2,1,0:T(8,128)(2,1)S(1)}, bf16[2,136,128]{2,1,0:T(8,128)(2,1)S(1)}, u32[]{:S(2)}, u32[]{:S(2)}) collective-permute-start(bf16[2,136,128]{2,1,0:T(8,128)(2,1)S(1)} %bitcast.4), channel_id=1, source_target_pairs={{0,0},{1,32},{2,8},{3,40},{4,16},{5,48},{6,24},{7,56},{8,200},{9,2... | collective-permute-start | bytes 208904 | tf_op jit(solution)/shard_map/ppermute | solution.py:117
  14.6 16.1 %copy-start.1 = (bf16[4,136,128]{2,1,0:T(8,128)(2,1)}, bf16[4,136,128]{2,1,0:T(8,128)(2,1)S(1)}, u32[]{:S(2)}) copy-start(bf16[4,136,128]{2,1,0:T(8,128)(2,1)S(1)} %all-gather.1) | copy-start | bytes 417796
  14.6 12.1 %collective-permute-start = (bf16[2,2,136,128]{3,2,1,0:T(8,128)(2,1)S(1)}, bf16[2,2,136,128]{3,2,1,0:T(8,128)(2,1)S(1)}, u32[]{:S(2)}, u32[]{:S(2)}) collective-permute-start(bf16[2,2,136,128]{3,2,1,0:T(8,128)(2,1)S(1)} %bitcast.6), channel_id=1, source_target_pairs={{0,2},{2,4},{4,6},{6,0},{1,3},{3,5},{5,7},{7,1},{8,10},{10,12},{12... | collective-permute-start | bytes 417800 | tf_op jit(solution)/shard_map/ppermute | solution.py:121
  14.6 16.1 %collective-permute-start.1 = (bf16[2,2,136,128]{3,2,1,0:T(8,128)(2,1)S(1)}, bf16[2,2,136,128]{3,2,1,0:T(8,128)(2,1)S(1)}, u32[]{:S(2)}, u32[]{:S(2)}) collective-permute-start(bf16[2,2,136,128]{3,2,1,0:T(8,128)(2,1)S(1)} %bitcast.7), channel_id=1, source_target_pairs={{0,6},{2,0},{4,2},{6,4},{1,7},{3,1},{5,3},{7,5},{8,14},{10,8},{12,... | collective-permute-start | bytes 417800 | tf_op jit(solution)/shard_map/ppermute | solution.py:121
  16.6 14.1 %collective-permute-start.2 = (bf16[2,2,136,128]{3,2,1,0:T(8,128)(2,1)S(1)}, bf16[2,2,136,128]{3,2,1,0:T(8,128)(2,1)S(1)}, u32[]{:S(2)}, u32[]{:S(2)}) collective-permute-start(bf16[2,2,136,128]{3,2,1,0:T(8,128)(2,1)S(1)} %bitcast.8), channel_id=1, source_target_pairs={{0,4},{2,6},{4,0},{6,2},{1,5},{3,7},{5,1},{7,3},{8,12},{10,14},{12... | collective-permute-start | bytes 417800 | tf_op jit(solution)/shard_map/ppermute | solution.py:121
  17.3 7.2 %collective-permute-start.4 = (bf16[2,136,128]{2,1,0:T(8,128)(2,1)S(1)}, bf16[2,136,128]{2,1,0:T(8,128)(2,1)S(1)}, u32[]{:S(2)}, u32[]{:S(2)}) collective-permute-start(bf16[2,136,128]{2,1,0:T(8,128)(2,1)S(1)} %collective-permute-done.3), channel_id=1, source_target_pairs={{0,64},{64,0},{1,65},{65,1},{2,66},{66,2},{3,67},{67,3},{4,68},{68... | collective-permute-start | bytes 208904 | tf_op jit(solution)/shard_map/ppermute | solution.py:122
  24.6 11.5 %copy-start = (bf16[2,2,136,128]{3,2,1,0:T(8,128)(2,1)}, bf16[2,2,136,128]{3,2,1,0:T(8,128)(2,1)S(1)}, u32[]{:S(2)}) copy-start(bf16[2,2,136,128]{3,2,1,0:T(8,128)(2,1)S(1)} %maximum_select_fusion.block) | copy-start | bytes 417796
  24.6 15.6 %collective-permute-start.7 = (bf16[2,2,136,128]{3,2,1,0:T(8,128)(2,1)S(1)}, bf16[2,2,136,128]{3,2,1,0:T(8,128)(2,1)S(1)}, u32[]{:S(2)}, u32[]{:S(2)}) collective-permute-start(bf16[2,2,136,128]{3,2,1,0:T(8,128)(2,1)S(1)} %maximum_select_fusion.block), channel_id=1, source_target_pairs={{0,8},{8,16},{16,24},{24,32},{32,40},{40,48},{48,56},{56,0},{1,9},... | collective-permute-start | bytes 417800 | tf_op jit(solution)/shard_map/ppermute | solution.py:127
  24.7 20.3 %collective-permute-start.6 = (bf16[2,2,136,128]{3,2,1,0:T(8,128)(2,1)S(1)}, bf16[2,2,136,128]{3,2,1,0:T(8,128)(2,1)S(1)}, u32[]{:S(2)}, u32[]{:S(2)}) collective-permute-start(bf16[2,2,136,128]{3,2,1,0:T(8,128)(2,1)S(1)} %maximum_select_fusion.block), channel_id=1, source_target_pairs={{0,56},{8,0},{16,8},{24,16},{32,24},{40,32},{48,40},{56,48},{1,57}... | collective-permute-start | bytes 417800 | tf_op jit(solution)/shard_map/ppermute | solution.py:127
  26.7 4.1 %copy-start.5 = (bf16[2,2,136,128]{3,2,1,0:T(8,128)(2,1)}, bf16[2,2,136,128]{3,2,1,0:T(8,128)(2,1)S(1)}, u32[]{:S(2)}) copy-start(bf16[2,2,136,128]{3,2,1,0:T(8,128)(2,1)S(1)} %collective-permute-done.before) | copy-start | bytes 417796
  26.7 23.1 %collective-permute-start.5 = (bf16[2,2,136,128]{3,2,1,0:T(8,128)(2,1)S(1)}, bf16[2,2,136,128]{3,2,1,0:T(8,128)(2,1)S(1)}, u32[]{:S(2)}, u32[]{:S(2)}) collective-permute-start(bf16[2,2,136,128]{3,2,1,0:T(8,128)(2,1)S(1)} %maximum_select_fusion.block), channel_id=1, source_target_pairs={{0,16},{8,56},{16,32},{24,8},{32,48},{40,24},{48,0},{56,40},{1,17}... | collective-permute-start | bytes 417800 | tf_op jit(solution)/shard_map/ppermute | solution.py:127
  30.7 0.6 %copy-start.6 = (bf16[2,2,136,128]{3,2,1,0:T(8,128)(2,1)}, bf16[2,2,136,128]{3,2,1,0:T(8,128)(2,1)S(1)}, u32[]{:S(2)}) copy-start(bf16[2,2,136,128]{3,2,1,0:T(8,128)(2,1)S(1)} %collective-permute-done.1.after) | copy-start | bytes 417796
  31.4 0.6 %copy-start.7 = (bf16[2,2,136,128]{3,2,1,0:T(8,128)(2,1)}, bf16[2,2,136,128]{3,2,1,0:T(8,128)(2,1)S(1)}, u32[]{:S(2)}) copy-start(bf16[2,2,136,128]{3,2,1,0:T(8,128)(2,1)S(1)} %collective-permute-done.2.across) | copy-start | bytes 417796
  40.2 0.7 %copy-start.4 = (bf16[2,2,136,128]{3,2,1,0:T(8,128)(2,1)}, bf16[2,2,136,128]{3,2,1,0:T(8,128)(2,1)S(1)}, u32[]{:S(2)}) copy-start(bf16[2,2,136,128]{3,2,1,0:T(8,128)(2,1)S(1)} %collective-permute-done.7.block) | copy-start | bytes 417796
  45.0 0.7 %copy-start.3 = (bf16[2,2,136,128]{3,2,1,0:T(8,128)(2,1)}, bf16[2,2,136,128]{3,2,1,0:T(8,128)(2,1)S(1)}, u32[]{:S(2)}) copy-start(bf16[2,2,136,128]{3,2,1,0:T(8,128)(2,1)S(1)} %collective-permute-done.6.block) | copy-start | bytes 417796
  49.8 0.7 %copy-start.2 = (bf16[2,2,136,128]{3,2,1,0:T(8,128)(2,1)}, bf16[2,2,136,128]{3,2,1,0:T(8,128)(2,1)S(1)}, u32[]{:S(2)}) copy-start(bf16[2,2,136,128]{3,2,1,0:T(8,128)(2,1)S(1)} %collective-permute-done.5.block) | copy-start | bytes 417796

commit v2 on v1

v2 whole, which is shorter than its diff:
```python
import functools
import itertools

import jax
import jax.numpy as jnp
from jax import lax
from jax.experimental import pallas as pl
from jax.experimental.pallas import tpu as pltpu
from jax.sharding import Mesh
from jax.sharding import PartitionSpec as P

AXES = ("yl", "yh", "zh", "zq", "x", "c")
SIZES = (2, 2, 2, 4, 4, 2)
LANES = 128
DEPTH = 256
EARLY = 72
CHUNK = 512
CALLS = (((0,), slice(0, 1)), ((3, 1, 2), slice(1, 4)))
PARAMS = pltpu.CompilerParams(vmem_limit_bytes=24 * 2**20)


def place(yl, yh, zh, zq, x, c):
    number = 0
    for size, index in zip(SIZES, (yl, yh, zh, zq, x, c)):
        number = number * size + index
    return number


def corner_turn():
    pairs = []
    for yl, yh, zh, zq, x, c in itertools.product(*map(range, SIZES)):
        to_x, to_c, to_yl = 2 * yh + zh, zq // 2, zq % 2
        to_yh = yh if yl == to_yl else 1 - yh
        to_zh = (c + zh + to_c + 1) % 2
        to = (to_yl, to_yh, to_zh, (zq + x - to_x) % 4, to_x, to_c)
        pairs.append((place(yl, yh, zh, zq, x, c), place(*to)))
    assert all(source != target for source, target in pairs)
    return pairs


def ring(size, step):
    return [(i, (i + step) % size) for i in range(size)]


def two_apart(size):
    return [(i, (i + 2 - 4 * (i % 2)) % size) for i in range(size)]


def days_by_assets(block):
    columns = [
        jnp.concatenate([block[h, c].astype(jnp.float32) for h in range(2)], axis=0) for c in range(2)
    ]
    return jnp.concatenate(columns, axis=1)


def total(series):
    return jnp.sum(series, axis=0, keepdims=True)


def statistics(series, width, lasts):
    wide = width.astype(jnp.float32)
    middle, early, late = series[EARLY:DEPTH], series[:EARLY], series[DEPTH:]
    first_middle, second_middle = total(middle), total(middle * middle)
    early_day = lax.broadcasted_iota(jnp.int32, early.shape, 0)
    late_day = lax.broadcasted_iota(jnp.int32, late.shape, 0) + DEPTH
    found = []
    for last in lasts:
        kept_early = jnp.where(early_day > last - width, early, 0.0)
        kept_late = jnp.where(late_day <= last, late, 0.0)
        first = first_middle + total(kept_early) + total(kept_late)
        second = second_middle + total(kept_early * kept_early) + total(kept_late * kept_late)
        found.append((first, lax.rsqrt((second - first * first / wide) / wide + 1e-06)))
    return found


def encoded(window, out_days):
    late = jnp.sum(lax.shift_left(out_days - (DEPTH - 1), 5 * jnp.arange(4, dtype=jnp.int32) + 9))
    return (window[0] + late).reshape(1)


def decoded(facts):
    code = facts[0]
    lasts = [(lax.shift_right_logical(code, 9 + 5 * k) & 31) + (DEPTH - 1) for k in range(4)]
    return code & 511, lasts


def prepare_rows(facts, own, before, after, across, low, high, spread):
    width, lasts = decoded(facts)
    x = lax.axis_index("x")
    for ref, step in ((own, 0), (before, 3), (after, 1), (across, 2)):
        quarter = lax.rem(x + step, 4)
        rows = pl.ds(pl.multiple_of(quarter * 256, 256), 256)
        series = days_by_assets(ref)
        days, assets = series.shape
        spare = days - DEPTH
        found = statistics(series, width, lasts)
        table = [first for first, _ in found] + [scale for _, scale in found]
        table.append(jnp.zeros((LANES - 8, assets), jnp.float32))
        stats = jnp.concatenate(table, axis=0).T
        for n in range(8):
            spread[n, rows, :] = jnp.broadcast_to(stats[:, n : n + 1], (assets, LANES))
        high[rows, :] = series[LANES:DEPTH].T.astype(jnp.bfloat16)
        main = series[:LANES].T
        folded = jnp.concatenate([series[DEPTH:], jnp.zeros((LANES - spare, assets), jnp.float32)], axis=0).T
        slot = lax.broadcasted_iota(jnp.int32, (assets, LANES), 1)
        for k, last in enumerate(lasts):
            left = jnp.where(slot > last - width, main, 0.0)
            left = jnp.where((slot < spare) & (slot + DEPTH <= last), folded, left)
            low[k, rows, :] = left.astype(jnp.bfloat16)


def correlate(steps, facts, low, high, spread, *refs):
    blocks, (out, result, sems) = refs[: len(steps)], refs[-3:]
    turn = lax.axis_index("x") + lax.axis_index("zq") - 2 * lax.axis_index("c") - lax.axis_index("yl")
    width, lasts = decoded(facts)
    wide = width.astype(jnp.float32)
    copies = []
    for n, (step, block) in enumerate(zip(steps, blocks)):
        columns = pl.ds(pl.multiple_of(lax.rem(turn + step + 8, 4) * 256, 256), 256)
        series = days_by_assets(block)
        spare = series.shape[0] - DEPTH
        common = series[spare:DEPTH].astype(jnp.bfloat16)
        for k, (first, scale) in enumerate(statistics(series, width, lasts)):
            mean, scale = first / wide, scale / wide
            slot = lax.broadcasted_iota(jnp.int32, (spare, series.shape[1]), 0)
            head = jnp.where(slot + DEPTH <= lasts[k], series[DEPTH:], series[:spare])
            right = jnp.concatenate([head.astype(jnp.bfloat16), common], axis=0)
            for i in range(low.shape[1] // CHUNK):
                rows = slice(i * CHUNK, (i + 1) * CHUNK)
                left = jnp.concatenate([low[k, rows, :], high[rows, :]], axis=1)
                gram = jnp.dot(left, right, preferred_element_type=jnp.float32)
                row_sum, row_scale = spread[k, rows, :], spread[4 + k, rows, :]
                for h in (slice(0, LANES), slice(LANES, 2 * LANES)):
                    cov = gram[:, h] - row_sum * mean[:, h]
                    result[n, k, rows, h] = (cov * row_scale * scale[:, h]).astype(jnp.bfloat16)
                copy = pltpu.make_async_copy(
                    result.at[n, k, rows], out.at[k, rows, columns], sems.at[n, k, i]
                )
                copy.start()
                copies.append(copy)
    for copy in copies:
        copy.wait()


def exchange_and_correlate(returns, window, out_days):
    facts = encoded(window, out_days)
    pair = lax.all_gather(returns, "c", axis=0)
    turned = lax.ppermute(pair, AXES, corner_turn())
    own_rows = lax.all_gather(pair, "yl", axis=0)
    turned, own_rows = lax.optimization_barrier((turned, own_rows))
    other = lax.ppermute(turned, "yh", ring(2, 1))
    rows = [own_rows]
    for links in (ring(4, 1), ring(4, 3), ring(4, 2)):
        rows.append(lax.ppermute(own_rows, "x", links))
    half = lax.axis_index("yl") + lax.axis_index("yh") + lax.axis_index("x") // 2
    own_columns = jnp.where(half % 2 == 0, jnp.stack([turned, other]), jnp.stack([other, turned]))
    columns = [own_columns]
    for links in (ring(8, 1), ring(8, 7), two_apart(8)):
        columns.append(lax.ppermute(own_columns, ("zh", "zq"), links))

    smem, vmem = pl.BlockSpec(memory_space=pltpu.SMEM), pl.BlockSpec(memory_space=pltpu.VMEM)
    anywhere = pl.BlockSpec(memory_space=pl.ANY)
    assets = 1024
    prepared = pl.pallas_call(
        prepare_rows,
        out_shape=(
            jax.ShapeDtypeStruct((4, assets, LANES), jnp.bfloat16),
            jax.ShapeDtypeStruct((assets, LANES), jnp.bfloat16),
            jax.ShapeDtypeStruct((8, assets, LANES), jnp.float32),
        ),
        in_specs=[smem] + [vmem] * 4,
        out_specs=(vmem, vmem, vmem),
        cost_estimate=pl.CostEstimate(flops=2_000_000_000, bytes_accessed=4_000_000, transcendentals=0),
        compiler_params=PARAMS,
        name="prepare_rows",
    )(facts, *rows)
    out = []
    for steps, blocks in CALLS:
        count = len(steps)
        out = [
            pl.pallas_call(
                functools.partial(correlate, steps),
                out_shape=jax.ShapeDtypeStruct((4, assets, assets), jnp.bfloat16),
                in_specs=[smem] + [vmem] * (3 + count) + [anywhere] * len(out),
                out_specs=anywhere,
                scratch_shapes=[
                    pltpu.VMEM((count, 4, assets, 256), jnp.bfloat16),
                    pltpu.SemaphoreType.DMA((count, 4, assets // CHUNK)),
                ],
                input_output_aliases={4 + count: 0} if out else {},
                cost_estimate=pl.CostEstimate(
                    flops=2_000_000_000 * count, bytes_accessed=2_000_000 * count, transcendentals=0
                ),
                compiler_params=PARAMS,
                name="correlate",
            )(facts, *prepared, *columns[blocks], *out)
        ]
    return out[0]


def solution(mesh):
    fine = Mesh(mesh.devices.reshape(SIZES), AXES)
    return jax.shard_map(
        exchange_and_correlate,
        mesh=fine,
        in_specs=(P("yl", ("yh", "zh", "zq", "x", "c")), P(), P()),
        out_specs=P(None, ("yh", "zh", "zq"), ("x", "c", "yl")),
        check_vma=False,
    )
```

time: 55 us -> 41.8 us (0.76)
  the two profiles are of different devices: /device:TPU:36 before, /device:TPU:2 now
where the time goes in v2:
time: 41.8 us; the launch traced here: 41.7 us
  starting transfers between devices  20.3 us (49%)
  Pallas kernels  8.57 us (21%)
  blocking collectives  7.57 us (18%)
  waiting for transfers between devices  2.28 us (5%)
  between operations  1.56 us (4%)
  other arithmetic  1.39 us (3%)
    ppermute x1, starting transfers between devices, exchange_and_correlate(): turned = lax.ppermute(pair, AXES, corner_turn())  6.77 us
    pallas_call x2, Pallas kernels, exchange_and_correlate(): pl.pallas_call(functools.partial(correlate, steps), out_shape=jax.ShapeDt...  6.62 us
    ppermute x3, starting transfers between devices, exchange_and_correlate(): columns.append(lax.ppermute(own_columns, ('zh', 'zq'), links))  6.47 us
    all_gather x1, blocking collectives, exchange_and_correlate(): own_rows = lax.all_gather(pair, 'yl', axis=0)  5.52 us
    ppermute x3, starting transfers between devices, exchange_and_correlate(): rows.append(lax.ppermute(own_rows, 'x', links))  4.06 us
    ppermute x1, starting transfers between devices, exchange_and_correlate(): other = lax.ppermute(turned, 'yh', ring(2, 1))  3.03 us
    ppermute x3, waiting for transfers between devices, exchange_and_correlate(): columns.append(lax.ppermute(own_columns, ('zh', 'zq'), links))  2.2 us
    all_gather x1, blocking collectives, exchange_and_correlate(): pair = lax.all_gather(returns, 'c', axis=0)  2.05 us
  transfers between devices with their start and end apart: 8, of which 2 were waited for; matrix products, arithmetic and copies ran while one was open for 3% of the time, Pallas kernels for 10%

profile of v2, /device:TPU:2, one launch (start us, length us, event | category | flops | bytes accessed | tf_op | source)
XLA Modules:
  0.0 41.7 jit_solution(17288501635004088329)
XLA Ops:
  0.0 2.1 %all-gather = bf16[272,128]{1,0:T(8,128)(2,1)S(1)} all-gather(bf16[136,128]{1,0:T(8,128)(2,1)} %param.3), channel_id=2, replica_groups=mesh['yl'=2,'yh'=2,'zh'=2,'zq'=4,'x'=4,'c'=2] {'c'}, dimensions={0}, use_global_device_ids=true | all-gather | bytes 104448 | tf_op jit(solution)/shard_map/all_gather | solution.py:147
  2.1 6.8 %collective-permute-start = (bf16[2,136,128]{2,1,0:T(8,128)(2,1)S(1)}, bf16[2,136,128]{2,1,0:T(8,128)(2,1)S(1)}, u32[]{:S(2)}, u32[]{:S(2)}) collective-permute-start(bf16[2,136,128]{2,1,0:T(8,128)(2,1)S(1)} %bitcast.11), channel_id=1, source_target_pairs={{0,32},{1,0},{2,40},{3,8},{4,48},{5,16},{6,56},{7,24},{8,232},{9,2... | collective-permute-start | bytes 208904 | tf_op jit(solution)/shard_map/ppermute | solution.py:148
  8.8 5.5 %all-gather.1 = bf16[4,136,128]{2,1,0:T(8,128)(2,1)S(1)} all-gather(bf16[2,136,128]{2,1,0:T(8,128)(2,1)S(1)} %bitcast.12), channel_id=3, replica_groups=mesh['yl'=2,'yh'=2,'zh'=2,'zq'=4,'x'=4,'c'=2] {'yl'}, dimensions={0}, use_global_device_ids=true | all-gather | bytes 208896 | tf_op jit(solution)/shard_map/all_gather | solution.py:149
  14.3 0.0 collective-permute-done
  14.3 2.0 %collective-permute-start.3 = (bf16[2,2,136,128]{3,2,1,0:T(8,128)(2,1)S(1)}, bf16[2,2,136,128]{3,2,1,0:T(8,128)(2,1)S(1)}, u32[]{:S(2)}, u32[]{:S(2)}) collective-permute-start(bf16[2,2,136,128]{3,2,1,0:T(8,128)(2,1)S(1)} %bitcast.7), channel_id=1, source_target_pairs={{0,4},{2,6},{4,0},{6,2},{1,5},{3,7},{5,1},{7,3},{8,12},{10,14},{12... | collective-permute-start | bytes 417800 | tf_op jit(solution)/shard_map/ppermute | solution.py:154
  16.4 1.1 %collective-permute-start.2 = (bf16[2,2,136,128]{3,2,1,0:T(8,128)(2,1)S(1)}, bf16[2,2,136,128]{3,2,1,0:T(8,128)(2,1)S(1)}, u32[]{:S(2)}, u32[]{:S(2)}) collective-permute-start(bf16[2,2,136,128]{3,2,1,0:T(8,128)(2,1)S(1)} %bitcast.8), channel_id=1, source_target_pairs={{0,6},{2,0},{4,2},{6,4},{1,7},{3,1},{5,3},{7,5},{8,14},{10,8},{12,... | collective-permute-start | bytes 417800 | tf_op jit(solution)/shard_map/ppermute | solution.py:154
  17.4 1.0 %collective-permute-start.1 = (bf16[2,2,136,128]{3,2,1,0:T(8,128)(2,1)S(1)}, bf16[2,2,136,128]{3,2,1,0:T(8,128)(2,1)S(1)}, u32[]{:S(2)}, u32[]{:S(2)}) collective-permute-start(bf16[2,2,136,128]{3,2,1,0:T(8,128)(2,1)S(1)} %bitcast.9), channel_id=1, source_target_pairs={{0,2},{2,4},{4,6},{6,0},{1,3},{3,5},{5,7},{7,1},{8,10},{10,12},{12... | collective-permute-start | bytes 417800 | tf_op jit(solution)/shard_map/ppermute | solution.py:154
  18.4 3.0 %collective-permute-start.4 = (bf16[2,136,128]{2,1,0:T(8,128)(2,1)S(1)}, bf16[2,136,128]{2,1,0:T(8,128)(2,1)S(1)}, u32[]{:S(2)}, u32[]{:S(2)}) collective-permute-start(bf16[2,136,128]{2,1,0:T(8,128)(2,1)S(1)} %collective-permute-done), channel_id=1, source_target_pairs={{0,64},{64,0},{1,65},{65,1},{2,66},{66,2},{3,67},{67,3},{4,68},{68... | collective-permute-start | bytes 208904 | tf_op jit(solution)/shard_map/ppermute | solution.py:151
  21.4 1.4 %shift-left_reduce_fusion = s32[]{:T(128)} fusion(s32[4]{0:T(128)} %param.5), kind=kLoop, calls=%fused_computation.1 | loop fusion | flops 19 | bytes 20 | tf_op jit(solution)/shard_map/reduce_sum | solution.py:77
  24.2 0.1 collective-permute-done.4
  24.2 2.1 %collective-permute-start.7 = (bf16[2,2,136,128]{3,2,1,0:T(8,128)(2,1)S(1)}, bf16[2,2,136,128]{3,2,1,0:T(8,128)(2,1)S(1)}, u32[]{:S(2)}, u32[]{:S(2)}) collective-permute-start(bf16[2,2,136,128]{3,2,1,0:T(8,128)(2,1)S(1)} %maximum_select_fusion.refs_0_), channel_id=1, source_target_pairs={{0,16},{8,56},{16,32},{24,8},{32,48},{40,24},{48,0},{56,40},{1,17}... | collective-permute-start | bytes 417800 | tf_op jit(solution)/shard_map/ppermute | solution.py:159
  26.4 4.3 %collective-permute-start.6 = (bf16[2,2,136,128]{3,2,1,0:T(8,128)(2,1)S(1)}, bf16[2,2,136,128]{3,2,1,0:T(8,128)(2,1)S(1)}, u32[]{:S(2)}, u32[]{:S(2)}) collective-permute-start(bf16[2,2,136,128]{3,2,1,0:T(8,128)(2,1)S(1)} %maximum_select_fusion.refs_0_), channel_id=1, source_target_pairs={{0,56},{8,0},{16,8},{24,16},{32,24},{40,32},{48,40},{56,48},{1,57}... | collective-permute-start | bytes 417800 | tf_op jit(solution)/shard_map/ppermute | solution.py:159
  30.7 0.0 collective-permute-done.3.across
  30.7 0.0 collective-permute-start.5
  30.7 0.0 collective-permute-done.2.after
  30.7 0.0 collective-permute-done.1.before
  30.7 2.0 %prepare_rows.1 = (bf16[4,1024,128]{2,1,0:T(8,128)(2,1)S(1)}, bf16[1024,128]{1,0:T(8,128)(2,1)S(1)}, f32[8,1024,128]{2,1,0:T(8,128)S(1)}) custom-call(s32[1]{0:T(128)} %bitcast.1.facts, bf16[2,2,136,128]{3,2,1,0:T(8,128)(2,1)S(1)} %bitcast.10, bf16[2,2,136,128]{3,2,1,0:T(8,128)(2,1)S(1)} %collective-permute-done.1.before, ...), custom_call_target="tpu_custom_call" | custom-call | flops 2000000000 | bytes 4000000 | tf_op jit(solution)/shard_map/prepare_rows/pallas_call | solution.py:164
  32.7 2.1 %correlate.2.refs_3_ = bf16[4,1024,1024]{2,1,0:T(8,128)(2,1)} custom-call(s32[1]{0:T(128)} %bitcast.1.facts, bf16[4,1024,128]{2,1,0:T(8,128)(2,1)S(1)} %get-tuple-element.11.low, bf16[1024,128]{1,0:T(8,128)(2,1)S(1)} %get-tuple-element.12.high, f32[8,1024,128]{2,1,0:T(8,128)S(1)} %get-tuple-element.13.spread, ...), custom_call_target="tpu_custom_call" | custom-call | flops 2000000000 | bytes 2000000 | tf_op jit(solution)/shard_map/correlate/pallas_call | solution.py:181
  34.8 0.0 collective-permute-done.7.refs_2_
  34.8 0.0 collective-permute-done.6.refs_1_
  34.8 2.2 %collective-permute-done.5.refs_0_ = bf16[2,2,136,128]{3,2,1,0:T(8,128)(2,1)S(1)} collective-permute-done((bf16[2,2,136,128]{3,2,1,0:T(8,128)(2,1)S(1)}, bf16[2,2,136,128]{3,2,1,0:T(8,128)(2,1)S(1)}, u32[]{:S(2)}, u32[]{:S(2)}) %collective-permute-start.5) | collective-permute-done | bytes 139296 | tf_op jit(solution)/shard_map/ppermute | solution.py:159
  37.0 4.6 %correlate.3 = bf16[4,1024,1024]{2,1,0:T(8,128)(2,1)} custom-call(s32[1]{0:T(128)} %bitcast.1.facts, bf16[4,1024,128]{2,1,0:T(8,128)(2,1)S(1)} %get-tuple-element.11.low, bf16[1024,128]{1,0:T(8,128)(2,1)S(1)} %get-tuple-element.12.high, f32[8,1024,128]{2,1,0:T(8,128)S(1)} %get-tuple-element.13.spread, ...), custom_call_target="tpu_custom_call", output_to_operand_aliasing={{}: (7, {})} | custom-call | flops 6000000000 | bytes 6000000 | tf_op jit(solution)/shard_map/correlate/pallas_call | solution.py:181
  (1 shorter events, 0.0 us)
Async XLA Ops:
  2.1 12.3 %collective-permute-start = (bf16[2,136,128]{2,1,0:T(8,128)(2,1)S(1)}, bf16[2,136,128]{2,1,0:T(8,128)(2,1)S(1)}, u32[]{:S(2)}, u32[]{:S(2)}) collective-permute-start(bf16[2,136,128]{2,1,0:T(8,128)(2,1)S(1)} %bitcast.11), channel_id=1, source_target_pairs={{0,32},{1,0},{2,40},{3,8},{4,48},{5,16},{6,56},{7,24},{8,232},{9,2... | collective-permute-start | bytes 208904 | tf_op jit(solution)/shard_map/ppermute | solution.py:148
  14.3 16.4 %collective-permute-start.3 = (bf16[2,2,136,128]{3,2,1,0:T(8,128)(2,1)S(1)}, bf16[2,2,136,128]{3,2,1,0:T(8,128)(2,1)S(1)}, u32[]{:S(2)}, u32[]{:S(2)}) collective-permute-start(bf16[2,2,136,128]{3,2,1,0:T(8,128)(2,1)S(1)} %bitcast.7), channel_id=1, source_target_pairs={{0,4},{2,6},{4,0},{6,2},{1,5},{3,7},{5,1},{7,3},{8,12},{10,14},{12... | collective-permute-start | bytes 417800 | tf_op jit(solution)/shard_map/ppermute | solution.py:154
  16.4 14.3 %collective-permute-start.2 = (bf16[2,2,136,128]{3,2,1,0:T(8,128)(2,1)S(1)}, bf16[2,2,136,128]{3,2,1,0:T(8,128)(2,1)S(1)}, u32[]{:S(2)}, u32[]{:S(2)}) collective-permute-start(bf16[2,2,136,128]{3,2,1,0:T(8,128)(2,1)S(1)} %bitcast.8), channel_id=1, source_target_pairs={{0,6},{2,0},{4,2},{6,4},{1,7},{3,1},{5,3},{7,5},{8,14},{10,8},{12,... | collective-permute-start | bytes 417800 | tf_op jit(solution)/shard_map/ppermute | solution.py:154
  17.4 13.3 %collective-permute-start.1 = (bf16[2,2,136,128]{3,2,1,0:T(8,128)(2,1)S(1)}, bf16[2,2,136,128]{3,2,1,0:T(8,128)(2,1)S(1)}, u32[]{:S(2)}, u32[]{:S(2)}) collective-permute-start(bf16[2,2,136,128]{3,2,1,0:T(8,128)(2,1)S(1)} %bitcast.9), channel_id=1, source_target_pairs={{0,2},{2,4},{4,6},{6,0},{1,3},{3,5},{5,7},{7,1},{8,10},{10,12},{12... | collective-permute-start | bytes 417800 | tf_op jit(solution)/shard_map/ppermute | solution.py:154
  18.4 5.8 %collective-permute-start.4 = (bf16[2,136,128]{2,1,0:T(8,128)(2,1)S(1)}, bf16[2,136,128]{2,1,0:T(8,128)(2,1)S(1)}, u32[]{:S(2)}, u32[]{:S(2)}) collective-permute-start(bf16[2,136,128]{2,1,0:T(8,128)(2,1)S(1)} %collective-permute-done), channel_id=1, source_target_pairs={{0,64},{64,0},{1,65},{65,1},{2,66},{66,2},{3,67},{67,3},{4,68},{68... | collective-permute-start | bytes 208904 | tf_op jit(solution)/shard_map/ppermute | solution.py:151
  24.2 10.5 %collective-permute-start.7 = (bf16[2,2,136,128]{3,2,1,0:T(8,128)(2,1)S(1)}, bf16[2,2,136,128]{3,2,1,0:T(8,128)(2,1)S(1)}, u32[]{:S(2)}, u32[]{:S(2)}) collective-permute-start(bf16[2,2,136,128]{3,2,1,0:T(8,128)(2,1)S(1)} %maximum_select_fusion.refs_0_), channel_id=1, source_target_pairs={{0,16},{8,56},{16,32},{24,8},{32,48},{40,24},{48,0},{56,40},{1,17}... | collective-permute-start | bytes 417800 | tf_op jit(solution)/shard_map/ppermute | solution.py:159
  26.4 8.4 %collective-permute-start.6 = (bf16[2,2,136,128]{3,2,1,0:T(8,128)(2,1)S(1)}, bf16[2,2,136,128]{3,2,1,0:T(8,128)(2,1)S(1)}, u32[]{:S(2)}, u32[]{:S(2)}) collective-permute-start(bf16[2,2,136,128]{3,2,1,0:T(8,128)(2,1)S(1)} %maximum_select_fusion.refs_0_), channel_id=1, source_target_pairs={{0,56},{8,0},{16,8},{24,16},{32,24},{40,32},{48,40},{56,48},{1,57}... | collective-permute-start | bytes 417800 | tf_op jit(solution)/shard_map/ppermute | solution.py:159
  30.7 6.3 %collective-permute-start.5 = (bf16[2,2,136,128]{3,2,1,0:T(8,128)(2,1)S(1)}, bf16[2,2,136,128]{3,2,1,0:T(8,128)(2,1)S(1)}, u32[]{:S(2)}, u32[]{:S(2)}) collective-permute-start(bf16[2,2,136,128]{3,2,1,0:T(8,128)(2,1)S(1)} %maximum_select_fusion.refs_0_), channel_id=1, source_target_pairs={{0,8},{8,16},{16,24},{24,32},{32,40},{40,48},{48,56},{56,0},{1,9},... | collective-permute-start | bytes 417800 | tf_op jit(solution)/shard_map/ppermute | solution.py:159

commit v3 on v2

v3 whole, which is shorter than its diff:
```python
import functools
import itertools

import jax
import jax.numpy as jnp
from jax import lax
from jax.experimental import pallas as pl
from jax.experimental.pallas import tpu as pltpu
from jax.sharding import Mesh
from jax.sharding import PartitionSpec as P

AXES = ("yl", "yh", "zh", "zq", "x", "c")
SIZES = (2, 2, 2, 4, 4, 2)
LANES = 128
DEPTH = 256
EARLY = 72
LATE = 16
CHUNK = 512
CALLS = (("across",), ("after", "before"))
PARAMS = pltpu.CompilerParams(vmem_limit_bytes=24 * 2**20)


def place(yl, yh, zh, zq, x, c):
    number = 0
    for size, index in zip(SIZES, (yl, yh, zh, zq, x, c)):
        number = number * size + index
    return number


def corner_turn():
    pairs = []
    for yl, yh, zh, zq, x, c in itertools.product(*map(range, SIZES)):
        to_x, to_c, to_yl = 2 * yh + zh, zq // 2, zq % 2
        to_yh = (yh + (yl != to_yl)) % 2
        to_zh = (c + zh + to_c + 1) % 2
        to = (to_yl, to_yh, to_zh, (zq + x - to_x) % 4, to_x, to_c)
        pairs.append((place(yl, yh, zh, zq, x, c), place(*to)))
    assert all(source != target for source, target in pairs)
    return pairs


def ring(size, step):
    return [(i, (i + step) % size) for i in range(size)]


def two_apart(size):
    return [(i, (i + 2 - 4 * (i % 2)) % size) for i in range(size)]


def write_masks(window, out_days, mask):
    width = window[0]
    early = lax.broadcasted_iota(jnp.int32, (EARLY, LANES), 0)
    late = lax.broadcasted_iota(jnp.int32, (LATE, LANES), 0) + DEPTH
    slot = lax.broadcasted_iota(jnp.int32, (1, LANES), 1)
    base = 4 * (EARLY + LATE)

    def one(test):
        return jnp.where(test, 1.0, 0.0).astype(jnp.float32)

    for k in range(4):
        last, start = out_days[k], k * (EARLY + LATE)
        mask[start : start + EARLY, :] = one(early > last - width)
        mask[start + EARLY : start + EARLY + LATE, :] = one(late <= last)
        mask[base + k : base + k + 1, :] = one(slot > last - width)
        mask[base + 4 + k : base + 5 + k, :] = one((slot < LATE) & (slot + DEPTH <= last))
    mask[base + 8 :, :] = jnp.full((8, LANES), width.astype(jnp.float32))


def twice(tile):
    return jnp.concatenate([tile, tile], axis=1)


def total(series):
    return jnp.sum(series, axis=0, keepdims=True)


def days_by_assets(block, half, chunk):
    columns = []
    for i in range(2):
        parts = [block[lax.rem(half + h, 2), lax.rem(chunk + i, 2)].astype(jnp.float32) for h in range(2)]
        columns.append(jnp.concatenate(parts, axis=0))
    return jnp.concatenate(columns, axis=1)


def by_day(mask, k):
    return mask[k * (EARLY + LATE) : (k + 1) * (EARLY + LATE), :]


def by_slot(mask, n):
    return mask[4 * (EARLY + LATE) + n : 4 * (EARLY + LATE) + n + 1, :]


def statistics(series, mask, wide):
    middle, early, late = series[EARLY:DEPTH], series[:EARLY], series[DEPTH:]
    first_middle, second_middle = total(middle), total(middle * middle)
    found = []
    for k in range(4):
        days = twice(by_day(mask, k))
        kept_early, kept_late = early * days[:EARLY], late * days[EARLY:]
        first = first_middle + total(kept_early) + total(kept_late)
        second = second_middle + total(kept_early * kept_early) + total(kept_late * kept_late)
        found.append((first, lax.rsqrt((second - first * first / wide) / wide + 1e-06)))
    return found


def along_lanes(table):
    high = table.astype(jnp.bfloat16)
    rest = table - high.astype(jnp.float32)
    middle = rest.astype(jnp.bfloat16)
    low = (rest - middle.astype(jnp.float32)).astype(jnp.bfloat16)
    parts = jnp.concatenate([part.astype(jnp.float32) for part in (high, middle, low)] + [jnp.zeros_like(table)], axis=0)
    row = lax.broadcasted_iota(jnp.int32, (4 * 8, 8 * LANES), 0)
    lane = lax.broadcasted_iota(jnp.int32, (4 * 8, 8 * LANES), 1)
    ones = jnp.where(row % 8 == lane // LANES, 1.0, 0.0).astype(jnp.bfloat16)
    return lax.dot_general(
        parts.astype(jnp.bfloat16), ones, (((0,), (0,)), ((), ())), preferred_element_type=jnp.float32
    )


def prepare_rows(mask, blocks, low, high, spread):
    x, c, yl = lax.axis_index("x"), lax.axis_index("c"), lax.axis_index("yl")
    wide = twice(by_slot(mask, 8))
    for step, block in zip((0, 3, 1, 2), blocks):
        rows = pl.ds(pl.multiple_of(lax.rem(x + step, 4) * 256, 256), 256)
        series = days_by_assets(block, yl, c)
        assets = series.shape[1]
        found = statistics(series, mask, wide)
        turned = along_lanes(jnp.concatenate([first for first, _ in found] + [scale for _, scale in found], axis=0))
        for i in range(8):
            spread[i, rows, :] = turned[:, i * LANES : (i + 1) * LANES]
        high[rows, :] = series[LANES:DEPTH].T.astype(jnp.bfloat16)
        main = series[:LANES].T
        folded = jnp.concatenate([series[DEPTH:], jnp.zeros((LANES - LATE, assets), jnp.float32)], axis=0).T
        for k in range(4):
            left = jnp.where(by_slot(mask, 4 + k) > 0.5, folded, main * by_slot(mask, k))
            low[k, rows, :] = left.astype(jnp.bfloat16)


def correlate(block, source, mask, low, high, spread, finish):
    x, c, yl, yh = (lax.axis_index(name) for name in ("x", "c", "yl", "yh"))
    z = 4 * lax.axis_index("zh") + lax.axis_index("zq")
    away = {"own": 0, "before": 7, "after": 1, "across": 6 - 4 * lax.rem(z, 2)}[source]
    half = lax.rem(yl + yh + x // 2, 2)
    from_core = lax.rem(lax.rem(z + away + 8, 8) // 4 + x + c + 1, 2)
    wide = twice(by_slot(mask, 8))
    series = days_by_assets(block, half, from_core)
    common = series[LATE:DEPTH].astype(jnp.bfloat16)
    for k, (first, scale) in enumerate(statistics(series, mask, wide)):
        mean, scale = first / wide, scale / wide
        head = jnp.where(twice(by_day(mask, k)[EARLY:]) > 0.5, series[DEPTH:], series[:LATE])
        right = jnp.concatenate([head.astype(jnp.bfloat16), common], axis=0)
        for i in range(low.shape[1] // CHUNK):
            rows = slice(i * CHUNK, (i + 1) * CHUNK)
            left = jnp.concatenate([low[k, rows, :], high[rows, :]], axis=1)
            gram = jnp.dot(left, right, preferred_element_type=jnp.float32)
            row_sum, row_scale = spread[k, rows, :], spread[4 + k, rows, :]
            tiles = []
            for h in (slice(0, LANES), slice(LANES, 2 * LANES)):
                cov = gram[:, h] - row_sum * mean[:, h]
                tiles.append((cov * row_scale * scale[:, h]).astype(jnp.bfloat16))
            finish(k, i, rows, tiles)


def columns_of(source):
    x, c, yl, zq = (lax.axis_index(name) for name in ("x", "c", "yl", "zq"))
    step = {"own": 0, "before": 3, "after": 1, "across": 2}[source]
    return pl.ds(pl.multiple_of(lax.rem(x + zq - 2 * c - yl + step + 8, 4) * 256, 256), 256)


def store(result, k, rows, tiles):
    for n, tile in enumerate(tiles):
        result[k, rows, n * LANES : (n + 1) * LANES] = tile


def begin(mask, own, before, after, across, own_block, low, high, spread, result):
    prepare_rows(mask, (own, before, after, across), low, high, spread)

    def finish(k, i, rows, tiles):
        store(result, k, rows, tiles)

    correlate(own_block, "own", mask, low, high, spread, finish)


def go_on(sources, ready, mask, low, high, spread, *refs):
    count = len(sources)
    blocks, (out, result, sems) = refs[:count], refs[-3:]
    copies = []

    def send(block, number, k, i, rows, source):
        copy = pltpu.make_async_copy(block.at[k, rows], out.at[k, rows, columns_of(source)], sems.at[number, k, i])
        copy.start()
        copies.append(copy)

    if ready is not None:
        for k in range(4):
            for i in range(low.shape[1] // CHUNK):
                send(refs[count], count, k, i, slice(i * CHUNK, (i + 1) * CHUNK), ready)
    for n, (source, block) in enumerate(zip(sources, blocks)):

        def finish(k, i, rows, tiles, n=n, source=source):
            store(result.at[n], k, rows, tiles)
            send(result.at[n], n, k, i, rows, source)

        correlate(block, source, mask, low, high, spread, finish)
    for copy in copies:
        copy.wait()


def exchange_and_correlate(returns, window, out_days):
    vmem, anywhere = pl.BlockSpec(memory_space=pltpu.VMEM), pl.BlockSpec(memory_space=pl.ANY)
    assets = 1024
    smem = pl.BlockSpec(memory_space=pltpu.SMEM)
    mask = pl.pallas_call(
        write_masks,
        out_shape=jax.ShapeDtypeStruct((4 * (EARLY + LATE) + 16, LANES), jnp.float32),
        in_specs=[smem, smem],
        out_specs=vmem,
        cost_estimate=pl.CostEstimate(flops=1_000_000_000, bytes_accessed=200_000, transcendentals=0),
        compiler_params=PARAMS,
        name="write_masks",
    )(window, out_days)
    pair = jnp.stack([returns, lax.ppermute(returns, "c", ring(2, 1))])
    turned = lax.ppermute(pair, AXES, corner_turn())
    own_rows = jnp.stack([pair, lax.ppermute(pair, "yl", ring(2, 1))])
    other = lax.ppermute(turned, "yh", ring(2, 1))
    rows = [own_rows]
    for links in (ring(4, 1), ring(4, 3), ring(4, 2)):
        rows.append(lax.ppermute(own_rows, "x", links))
    own = jnp.stack([turned, other])
    quarters = {"own": own}
    for source, links in (("before", ring(8, 1)), ("after", ring(8, 7)), ("across", two_apart(8))):
        quarters[source] = lax.ppermute(own, ("zh", "zq"), links)

    *prepared, own_result = pl.pallas_call(
        begin,
        out_shape=(
            jax.ShapeDtypeStruct((4, assets, LANES), jnp.bfloat16),
            jax.ShapeDtypeStruct((assets, LANES), jnp.bfloat16),
            jax.ShapeDtypeStruct((8, assets, LANES), jnp.float32),
            jax.ShapeDtypeStruct((4, assets, 256), jnp.bfloat16),
        ),
        in_specs=[vmem] * 6,
        out_specs=(vmem,) * 4,
        cost_estimate=pl.CostEstimate(flops=4_000_000_000, bytes_accessed=4_000_000, transcendentals=0),
        compiler_params=PARAMS,
        name="begin",
    )(mask, *rows, own)
    out, ready = [], "own"
    for sources in CALLS:
        count = len(sources)
        held = [] if ready is None else [own_result]
        out = [
            pl.pallas_call(
                functools.partial(go_on, sources, ready),
                out_shape=jax.ShapeDtypeStruct((4, assets, assets), jnp.bfloat16),
                in_specs=[vmem] * (4 + count + len(held)) + [anywhere] * len(out),
                out_specs=anywhere,
                scratch_shapes=[
                    pltpu.VMEM((count, 4, assets, 256), jnp.bfloat16),
                    pltpu.SemaphoreType.DMA((count + len(held), 4, assets // CHUNK)),
                ],
                input_output_aliases={4 + count: 0} if out else {},
                cost_estimate=pl.CostEstimate(
                    flops=2_000_000_000 * count, bytes_accessed=2_000_000 * count, transcendentals=0
                ),
                compiler_params=PARAMS,
                name="go_on",
            )(mask, *prepared, *[quarters[source] for source in sources], *held, *out)
        ]
        ready = None
    return out[0]


def solution(mesh):
    fine = Mesh(mesh.devices.reshape(SIZES), AXES)
    return jax.shard_map(
        exchange_and_correlate,
        mesh=fine,
        in_specs=(P("yl", ("yh", "zh", "zq", "x", "c")), P(), P()),
        out_specs=P(None, ("yh", "zh", "zq"), ("x", "c", "yl")),
        check_vma=False,
    )
```

time: 41.8 us -> 37.3 us (0.89)
  the two profiles are of different devices: /device:TPU:2 before, /device:TPU:4 now
where the time goes in v3:
time: 37.3 us; the launch traced here: 37.1 us
  starting transfers between devices  24.5 us (66%)
  Pallas kernels  7.79 us (21%)
  waiting for transfers between devices  2.5 us (7%)
  between operations  0.88 us (2%)
  other arithmetic  0.8 us (2%)
  local copies, waits for them, and re-layouts  0.65 us (2%)
    ppermute x3, starting transfers between devices, exchange_and_correlate(): quarters[source] = lax.ppermute(own, ('zh', 'zq'), links)  8.48 us
    ppermute x1, starting transfers between devices, exchange_and_correlate(): turned = lax.ppermute(pair, AXES, corner_turn())  6.33 us
    pallas_call x2, Pallas kernels, exchange_and_correlate(): pl.pallas_call(functools.partial(go_on, sources, ready), out_shape=jax.Sh...  5.28 us
    ppermute x1, starting transfers between devices, exchange_and_correlate(): other = lax.ppermute(turned, 'yh', ring(2, 1))  4.47 us
    ppermute x3, starting transfers between devices, exchange_and_correlate(): rows.append(lax.ppermute(own_rows, 'x', links))  3.57 us
    pallas_call x1, Pallas kernels, exchange_and_correlate(): pl.pallas_call(begin, out_shape=(jax.ShapeDtypeStruct((4, assets, LANES),...  1.95 us
    ppermute x1, starting transfers between devices, exchange_and_correlate(): own_rows = jnp.stack([pair, lax.ppermute(pair, 'yl', ring(2, 1))])  1.66 us
    ppermute x1, waiting for transfers between devices, exchange_and_correlate(): pair = jnp.stack([returns, lax.ppermute(returns, 'c', ring(2, 1))])  1.42 us
  transfers between devices with their start and end apart: 10, of which 2 were waited for; matrix products, arithmetic and copies ran while one was open for 0% of the time, Pallas kernels for 13%

profile of v3, /device:TPU:4, one launch (start us, length us, event | category | flops | bytes accessed | tf_op | source)
XLA Modules:
  0.0 37.1 jit_solution(3613354567115099680)
XLA Ops:
  0.0 0.0 collective-permute-start
  0.0 1.4 %collective-permute-done = bf16[136,128]{1,0:T(8,128)(2,1)S(1)} collective-permute-done((bf16[136,128]{1,0:T(8,128)(2,1)}, bf16[136,128]{1,0:T(8,128)(2,1)S(1)}, u32[]{:S(2)}, u32[]{:S(2)}) %collective-permute-start) | collective-permute-done | bytes 34848 | tf_op jit(solution)/shard_map/ppermute | solution.py:222
  1.4 0.8 %fusion = (bf16[1,2,136,128]{3,2,1,0:T(8,128)(2,1)S(1)}, bf16[2,136,128]{2,1,0:T(8,128)(2,1)S(1)}) fusion(bf16[1,136,128]{2,1,0:T(8,128)(2,1)S(1)} %bitcast.11, bf16[1,136,128]{2,1,0:T(8,128)(2,1)} %bitcast.10), kind=kLoop, calls=%fused_computation.3 | loop fusion | flops 34816 | bytes 208896 | tf_op jit(solution)/shard_map/stack | solution.py:224
  2.2 1.7 %collective-permute-start.1 = (bf16[2,136,128]{2,1,0:T(8,128)(2,1)S(1)}, bf16[2,136,128]{2,1,0:T(8,128)(2,1)S(1)}, u32[]{:S(2)}, u32[]{:S(2)}) collective-permute-start(bf16[2,136,128]{2,1,0:T(8,128)(2,1)S(1)} %get-tuple-element.14), channel_id=1, source_target_pairs={{0,128},{128,0},{1,129},{129,1},{2,130},{130,2},{3,131},{131,3},{4... | collective-permute-start | bytes 208904 | tf_op jit(solution)/shard_map/ppermute | solution.py:224
  4.5 6.3 %collective-permute-start.5 = (bf16[2,136,128]{2,1,0:T(8,128)(2,1)S(1)}, bf16[2,136,128]{2,1,0:T(8,128)(2,1)S(1)}, u32[]{:S(2)}, u32[]{:S(2)}) collective-permute-start(bf16[2,136,128]{2,1,0:T(8,128)(2,1)S(1)} %get-tuple-element.14), channel_id=1, source_target_pairs={{0,32},{1,0},{2,40},{3,8},{4,48},{5,16},{6,56},{7,24},{8,232},{9,2... | collective-permute-start | bytes 208904 | tf_op jit(solution)/shard_map/ppermute | solution.py:223
  10.8 0.0 collective-permute-done.1
  10.9 1.5 %collective-permute-start.4 = (bf16[2,2,136,128]{3,2,1,0:T(8,128)(2,1)S(1)}, bf16[2,2,136,128]{3,2,1,0:T(8,128)(2,1)S(1)}, u32[]{:S(2)}, u32[]{:S(2)}) collective-permute-start(bf16[2,2,136,128]{3,2,1,0:T(8,128)(2,1)S(1)} %pad_maximum_fusion.own), channel_id=1, source_target_pairs={{0,4},{2,6},{4,0},{6,2},{1,5},{3,7},{5,1},{7,3},{8,12},{10,14},{12... | collective-permute-start | bytes 417800 | tf_op jit(solution)/shard_map/ppermute | solution.py:228
  12.4 0.7 %collective-permute-start.3 = (bf16[2,2,136,128]{3,2,1,0:T(8,128)(2,1)S(1)}, bf16[2,2,136,128]{3,2,1,0:T(8,128)(2,1)S(1)}, u32[]{:S(2)}, u32[]{:S(2)}) collective-permute-start(bf16[2,2,136,128]{3,2,1,0:T(8,128)(2,1)S(1)} %pad_maximum_fusion.own), channel_id=1, source_target_pairs={{0,6},{2,0},{4,2},{6,4},{1,7},{3,1},{5,3},{7,5},{8,14},{10,8},{12,... | collective-permute-start | bytes 417800 | tf_op jit(solution)/shard_map/ppermute | solution.py:228
  13.1 1.3 %collective-permute-start.2 = (bf16[2,2,136,128]{3,2,1,0:T(8,128)(2,1)S(1)}, bf16[2,2,136,128]{3,2,1,0:T(8,128)(2,1)S(1)}, u32[]{:S(2)}, u32[]{:S(2)}) collective-permute-start(bf16[2,2,136,128]{3,2,1,0:T(8,128)(2,1)S(1)} %pad_maximum_fusion.own), channel_id=1, source_target_pairs={{0,2},{2,4},{4,6},{6,0},{1,3},{3,5},{5,7},{7,1},{8,10},{10,12},{12... | collective-permute-start | bytes 417800 | tf_op jit(solution)/shard_map/ppermute | solution.py:228
  14.4 0.0 collective-permute-done.5
  14.4 4.5 %collective-permute-start.6 = (bf16[2,136,128]{2,1,0:T(8,128)(2,1)S(1)}, bf16[2,136,128]{2,1,0:T(8,128)(2,1)S(1)}, u32[]{:S(2)}, u32[]{:S(2)}) collective-permute-start(bf16[2,136,128]{2,1,0:T(8,128)(2,1)S(1)} %collective-permute-done.5), channel_id=1, source_target_pairs={{0,64},{64,0},{1,65},{65,1},{2,66},{66,2},{3,67},{67,3},{4,68},{68... | collective-permute-start | bytes 208904 | tf_op jit(solution)/shard_map/ppermute | solution.py:225
  18.9 0.7 %copy-done = s32[4]{0:T(128)S(1)} copy-done((s32[4]{0:T(128)S(1)}, s32[4]{0:T(128)}, u32[]{:S(2)}) %copy-start) | copy-done | bytes 40
  19.6 0.6 %write_masks.1.mask = f32[368,128]{1,0:T(8,128)S(1)} custom-call(s32[1]{0:T(128)S(6)} %copy.6.window, s32[4]{0:T(128)S(1)} %copy-done), custom_call_target="tpu_custom_call" | custom-call | flops 1000000000 | bytes 200000 | tf_op jit(solution)/shard_map/write_masks/pallas_call | solution.py:213
  20.1 1.1 %collective-permute-done.6 = bf16[2,136,128]{2,1,0:T(8,128)(2,1)S(1)} collective-permute-done((bf16[2,136,128]{2,1,0:T(8,128)(2,1)S(1)}, bf16[2,136,128]{2,1,0:T(8,128)(2,1)S(1)}, u32[]{:S(2)}, u32[]{:S(2)}) %collective-permute-start.6) | collective-permute-done | bytes 69664 | tf_op jit(solution)/shard_map/ppermute | solution.py:225
  21.2 1.8 %collective-permute-start.9 = (bf16[2,2,136,128]{3,2,1,0:T(8,128)(2,1)S(1)}, bf16[2,2,136,128]{3,2,1,0:T(8,128)(2,1)S(1)}, u32[]{:S(2)}, u32[]{:S(2)}) collective-permute-start(bf16[2,2,136,128]{3,2,1,0:T(8,128)(2,1)S(1)} %pad_maximum_fusion.1.own_block), channel_id=1, source_target_pairs={{0,16},{8,56},{16,32},{24,8},{32,48},{40,24},{48,0},{56,40},{1,17}... | collective-permute-start | bytes 417800 | tf_op jit(solution)/shard_map/ppermute | solution.py:232
  23.0 4.4 %collective-permute-start.8 = (bf16[2,2,136,128]{3,2,1,0:T(8,128)(2,1)S(1)}, bf16[2,2,136,128]{3,2,1,0:T(8,128)(2,1)S(1)}, u32[]{:S(2)}, u32[]{:S(2)}) collective-permute-start(bf16[2,2,136,128]{3,2,1,0:T(8,128)(2,1)S(1)} %pad_maximum_fusion.1.own_block), channel_id=1, source_target_pairs={{0,8},{8,16},{16,24},{24,32},{32,40},{40,48},{48,56},{56,0},{1,9},... | collective-permute-start | bytes 417800 | tf_op jit(solution)/shard_map/ppermute | solution.py:232
  27.4 0.0 collective-permute-done.4.across
  27.4 2.3 %collective-permute-start.7 = (bf16[2,2,136,128]{3,2,1,0:T(8,128)(2,1)S(1)}, bf16[2,2,136,128]{3,2,1,0:T(8,128)(2,1)S(1)}, u32[]{:S(2)}, u32[]{:S(2)}) collective-permute-start(bf16[2,2,136,128]{3,2,1,0:T(8,128)(2,1)S(1)} %pad_maximum_fusion.1.own_block), channel_id=1, source_target_pairs={{0,56},{8,0},{16,8},{24,16},{32,24},{40,32},{48,40},{56,48},{1,57}... | collective-permute-start | bytes 417800 | tf_op jit(solution)/shard_map/ppermute | solution.py:232
  29.7 0.0 collective-permute-done.3.after
  29.7 0.0 collective-permute-done.2.before
  29.7 2.0 %begin.1 = (bf16[4,1024,128]{2,1,0:T(8,128)(2,1)S(1)}, bf16[1024,128]{1,0:T(8,128)(2,1)S(1)}, f32[8,1024,128]{2,1,0:T(8,128)S(1)}, bf16[4,1024,256]{2,1,0:T(8,128)(2,1)S(1)}) custom-call(f32[368,128]{1,0:T(8,128)S(1)} %write_masks.1.mask, bf16[2,2,136,128]{3,2,1,0:T(8,128)(2,1)S(1)} %pad_maximum_fusion.own, ...), custom_call_target="tpu_custom_call" | custom-call | flops 4000000000 | bytes 4000000 | tf_op jit(solution)/shard_map/begin/pallas_call | solution.py:234
  31.7 0.0 collective-permute-done.9.refs_0_
  31.7 2.2 %go_on.2.refs_2_ = bf16[4,1024,1024]{2,1,0:T(8,128)(2,1)} custom-call(f32[368,128]{1,0:T(8,128)S(1)} %write_masks.1.mask, bf16[4,1024,128]{2,1,0:T(8,128)(2,1)S(1)} %get-tuple-element.9.low, bf16[1024,128]{1,0:T(8,128)(2,1)S(1)} %get-tuple-element.10.high, f32[8,1024,128]{2,1,0:T(8,128)S(1)} %get-tuple-element.11.spread, ...), custom_call_target="tpu_custom_call" | custom-call | flops 2000000000 | bytes 2000000 | tf_op jit(solution)/shard_map/go_on/pallas_call | solution.py:253
  33.9 3.1 %go_on.3 = bf16[4,1024,1024]{2,1,0:T(8,128)(2,1)} custom-call(f32[368,128]{1,0:T(8,128)S(1)} %write_masks.1.mask, bf16[4,1024,128]{2,1,0:T(8,128)(2,1)S(1)} %get-tuple-element.9.low, bf16[1024,128]{1,0:T(8,128)(2,1)S(1)} %get-tuple-element.10.high, f32[8,1024,128]{2,1,0:T(8,128)S(1)} %get-tuple-element.11.spread, ...), custom_call_target="tpu_custom_call", output_to_operand_aliasing={{}: (6, {})} | custom-call | flops 4000000000 | bytes 4000000 | tf_op jit(solution)/shard_map/go_on/pallas_call | solution.py:253
  (5 shorter events, 0.0 us)
Async XLA Ops:
  0.0 1.4 %collective-permute-start = (bf16[136,128]{1,0:T(8,128)(2,1)}, bf16[136,128]{1,0:T(8,128)(2,1)S(1)}, u32[]{:S(2)}, u32[]{:S(2)}) collective-permute-start(bf16[136,128]{1,0:T(8,128)(2,1)} %param.3), channel_id=1, source_target_pairs={{0,1},{1,0},{2,3},{3,2},{4,5},{5,4},{6,7},{7,6},{8,9},{9,8},{10,11... | collective-permute-start | bytes 104456 | tf_op jit(solution)/shard_map/ppermute | solution.py:222
  2.2 8.6 %collective-permute-start.1 = (bf16[2,136,128]{2,1,0:T(8,128)(2,1)S(1)}, bf16[2,136,128]{2,1,0:T(8,128)(2,1)S(1)}, u32[]{:S(2)}, u32[]{:S(2)}) collective-permute-start(bf16[2,136,128]{2,1,0:T(8,128)(2,1)S(1)} %get-tuple-element.14), channel_id=1, source_target_pairs={{0,128},{128,0},{1,129},{129,1},{2,130},{130,2},{3,131},{131,3},{4... | collective-permute-start | bytes 208904 | tf_op jit(solution)/shard_map/ppermute | solution.py:224
  4.5 9.9 %collective-permute-start.5 = (bf16[2,136,128]{2,1,0:T(8,128)(2,1)S(1)}, bf16[2,136,128]{2,1,0:T(8,128)(2,1)S(1)}, u32[]{:S(2)}, u32[]{:S(2)}) collective-permute-start(bf16[2,136,128]{2,1,0:T(8,128)(2,1)S(1)} %get-tuple-element.14), channel_id=1, source_target_pairs={{0,32},{1,0},{2,40},{3,8},{4,48},{5,16},{6,56},{7,24},{8,232},{9,2... | collective-permute-start | bytes 208904 | tf_op jit(solution)/shard_map/ppermute | solution.py:223
  10.9 16.5 %collective-permute-start.4 = (bf16[2,2,136,128]{3,2,1,0:T(8,128)(2,1)S(1)}, bf16[2,2,136,128]{3,2,1,0:T(8,128)(2,1)S(1)}, u32[]{:S(2)}, u32[]{:S(2)}) collective-permute-start(bf16[2,2,136,128]{3,2,1,0:T(8,128)(2,1)S(1)} %pad_maximum_fusion.own), channel_id=1, source_target_pairs={{0,4},{2,6},{4,0},{6,2},{1,5},{3,7},{5,1},{7,3},{8,12},{10,14},{12... | collective-permute-start | bytes 417800 | tf_op jit(solution)/shard_map/ppermute | solution.py:228
  12.4 17.3 %collective-permute-start.3 = (bf16[2,2,136,128]{3,2,1,0:T(8,128)(2,1)S(1)}, bf16[2,2,136,128]{3,2,1,0:T(8,128)(2,1)S(1)}, u32[]{:S(2)}, u32[]{:S(2)}) collective-permute-start(bf16[2,2,136,128]{3,2,1,0:T(8,128)(2,1)S(1)} %pad_maximum_fusion.own), channel_id=1, source_target_pairs={{0,6},{2,0},{4,2},{6,4},{1,7},{3,1},{5,3},{7,5},{8,14},{10,8},{12,... | collective-permute-start | bytes 417800 | tf_op jit(solution)/shard_map/ppermute | solution.py:228
  13.1 16.6 %collective-permute-start.2 = (bf16[2,2,136,128]{3,2,1,0:T(8,128)(2,1)S(1)}, bf16[2,2,136,128]{3,2,1,0:T(8,128)(2,1)S(1)}, u32[]{:S(2)}, u32[]{:S(2)}) collective-permute-start(bf16[2,2,136,128]{3,2,1,0:T(8,128)(2,1)S(1)} %pad_maximum_fusion.own), channel_id=1, source_target_pairs={{0,2},{2,4},{4,6},{6,0},{1,3},{3,5},{5,7},{7,1},{8,10},{10,12},{12... | collective-permute-start | bytes 417800 | tf_op jit(solution)/shard_map/ppermute | solution.py:228
  14.4 6.8 %collective-permute-start.6 = (bf16[2,136,128]{2,1,0:T(8,128)(2,1)S(1)}, bf16[2,136,128]{2,1,0:T(8,128)(2,1)S(1)}, u32[]{:S(2)}, u32[]{:S(2)}) collective-permute-start(bf16[2,136,128]{2,1,0:T(8,128)(2,1)S(1)} %collective-permute-done.5), channel_id=1, source_target_pairs={{0,64},{64,0},{1,65},{65,1},{2,66},{66,2},{3,67},{67,3},{4,68},{68... | collective-permute-start | bytes 208904 | tf_op jit(solution)/shard_map/ppermute | solution.py:225
  18.9 0.7 %copy-start = (s32[4]{0:T(128)S(1)}, s32[4]{0:T(128)}, u32[]{:S(2)}) copy-start(s32[4]{0:T(128)} %out_days.1) | copy-start | bytes 52
  21.2 10.5 %collective-permute-start.9 = (bf16[2,2,136,128]{3,2,1,0:T(8,128)(2,1)S(1)}, bf16[2,2,136,128]{3,2,1,0:T(8,128)(2,1)S(1)}, u32[]{:S(2)}, u32[]{:S(2)}) collective-permute-start(bf16[2,2,136,128]{3,2,1,0:T(8,128)(2,1)S(1)} %pad_maximum_fusion.1.own_block), channel_id=1, source_target_pairs={{0,16},{8,56},{16,32},{24,8},{32,48},{40,24},{48,0},{56,40},{1,17}... | collective-permute-start | bytes 417800 | tf_op jit(solution)/shard_map/ppermute | solution.py:232
  23.0 10.9 %collective-permute-start.8 = (bf16[2,2,136,128]{3,2,1,0:T(8,128)(2,1)S(1)}, bf16[2,2,136,128]{3,2,1,0:T(8,128)(2,1)S(1)}, u32[]{:S(2)}, u32[]{:S(2)}) collective-permute-start(bf16[2,2,136,128]{3,2,1,0:T(8,128)(2,1)S(1)} %pad_maximum_fusion.1.own_block), channel_id=1, source_target_pairs={{0,8},{8,16},{16,24},{24,32},{32,40},{40,48},{48,56},{56,0},{1,9},... | collective-permute-start | bytes 417800 | tf_op jit(solution)/shard_map/ppermute | solution.py:232
  27.4 6.5 %collective-permute-start.7 = (bf16[2,2,136,128]{3,2,1,0:T(8,128)(2,1)S(1)}, bf16[2,2,136,128]{3,2,1,0:T(8,128)(2,1)S(1)}, u32[]{:S(2)}, u32[]{:S(2)}) collective-permute-start(bf16[2,2,136,128]{3,2,1,0:T(8,128)(2,1)S(1)} %pad_maximum_fusion.1.own_block), channel_id=1, source_target_pairs={{0,56},{8,0},{16,8},{24,16},{32,24},{40,32},{48,40},{56,48},{1,57}... | collective-permute-start | bytes 417800 | tf_op jit(solution)/shard_map/ppermute | solution.py:232

commit v4 on v3

--- a/solution.py
+++ b/solution.py
@@ -16,7 +16,8 @@
 EARLY = 72
 LATE = 16
 CHUNK = 512
-CALLS = (("across",), ("after", "before"))
+ORDER = ("before", "across", "after")
+CALLS = (ORDER[:1], ORDER[1:])
 PARAMS = pltpu.CompilerParams(vmem_limit_bytes=24 * 2**20)
 
 
@@ -74,10 +75,10 @@
     return jnp.sum(series, axis=0, keepdims=True)
 
 
-def days_by_assets(block, half, chunk):
+def days_by_assets(block, half):
     columns = []
-    for i in range(2):
-        parts = [block[lax.rem(half + h, 2), lax.rem(chunk + i, 2)].astype(jnp.float32) for h in range(2)]
+    for chunk in range(2):
+        parts = [block[lax.rem(half + h, 2), chunk].astype(jnp.float32) for h in range(2)]
         columns.append(jnp.concatenate(parts, axis=0))
     return jnp.concatenate(columns, axis=1)
 
@@ -118,11 +119,11 @@
 
 
 def prepare_rows(mask, blocks, low, high, spread):
-    x, c, yl = lax.axis_index("x"), lax.axis_index("c"), lax.axis_index("yl")
+    x, yl = lax.axis_index("x"), lax.axis_index("yl")
     wide = twice(by_slot(mask, 8))
     for step, block in zip((0, 3, 1, 2), blocks):
         rows = pl.ds(pl.multiple_of(lax.rem(x + step, 4) * 256, 256), 256)
-        series = days_by_assets(block, yl, c)
+        series = days_by_assets(block, yl)
         assets = series.shape[1]
         found = statistics(series, mask, wide)
         turned = along_lanes(jnp.concatenate([first for first, _ in found] + [scale for _, scale in found], axis=0))
@@ -136,14 +137,10 @@
             low[k, rows, :] = left.astype(jnp.bfloat16)
 
 
-def correlate(block, source, mask, low, high, spread, finish):
-    x, c, yl, yh = (lax.axis_index(name) for name in ("x", "c", "yl", "yh"))
-    z = 4 * lax.axis_index("zh") + lax.axis_index("zq")
-    away = {"own": 0, "before": 7, "after": 1, "across": 6 - 4 * lax.rem(z, 2)}[source]
-    half = lax.rem(yl + yh + x // 2, 2)
-    from_core = lax.rem(lax.rem(z + away + 8, 8) // 4 + x + c + 1, 2)
+def correlate(block, mask, low, high, spread, finish):
+    half = lax.rem(lax.axis_index("yl") + lax.axis_index("yh") + lax.axis_index("x") // 2, 2)
     wide = twice(by_slot(mask, 8))
-    series = days_by_assets(block, half, from_core)
+    series = days_by_assets(block, half)
     common = series[LATE:DEPTH].astype(jnp.bfloat16)
     for k, (first, scale) in enumerate(statistics(series, mask, wide)):
         mean, scale = first / wide, scale / wide
@@ -178,12 +175,13 @@
     def finish(k, i, rows, tiles):
         store(result, k, rows, tiles)
 
-    correlate(own_block, "own", mask, low, high, spread, finish)
-
-
-def go_on(sources, ready, mask, low, high, spread, *refs):
+    correlate(own_block, mask, low, high, spread, finish)
+
+
+def go_on(sources, ready, kept, mask, low, high, spread, *refs):
     count = len(sources)
-    blocks, (out, result, sems) = refs[:count], refs[-3:]
+    blocks, held, out = refs[:count], refs[count], refs[-3 - (kept is not None)]
+    result, sems = refs[-2:]
     copies = []
 
     def send(block, number, k, i, rows, source):
@@ -191,17 +189,24 @@
         copy.start()
         copies.append(copy)
 
-    if ready is not None:
-        for k in range(4):
-            for i in range(low.shape[1] // CHUNK):
-                send(refs[count], count, k, i, slice(i * CHUNK, (i + 1) * CHUNK), ready)
-    for n, (source, block) in enumerate(zip(sources, blocks)):
-
-        def finish(k, i, rows, tiles, n=n, source=source):
-            store(result.at[n], k, rows, tiles)
-            send(result.at[n], n, k, i, rows, source)
-
-        correlate(block, source, mask, low, high, spread, finish)
+    for k in range(4):
+        for i in range(low.shape[1] // CHUNK):
+            send(held, count, k, i, slice(i * CHUNK, (i + 1) * CHUNK), ready)
+
+    def work():
+        for n, (source, block) in enumerate(zip(sources, blocks)):
+
+            def finish(k, i, rows, tiles, n=n, source=source):
+                store(refs[-3] if source == kept else result.at[n], k, rows, tiles)
+                if source != kept:
+                    send(result.at[n], n, k, i, rows, source)
+
+            correlate(block, mask, low, high, spread, finish)
+
+    if kept is None:
+        work()
+    else:
+        pl.when(lax.axis_index("x") >= 0)(work)
     for copy in copies:
         copy.wait()
 
@@ -219,7 +224,7 @@
         compiler_params=PARAMS,
         name="write_masks",
     )(window, out_days)
-    pair = jnp.stack([returns, lax.ppermute(returns, "c", ring(2, 1))])
+    pair = lax.all_gather(returns, "c", axis=0)
     turned = lax.ppermute(pair, AXES, corner_turn())
     own_rows = jnp.stack([pair, lax.ppermute(pair, "yl", ring(2, 1))])
     other = lax.ppermute(turned, "yh", ring(2, 1))
@@ -245,29 +250,28 @@
         compiler_params=PARAMS,
         name="begin",
     )(mask, *rows, own)
-    out, ready = [], "own"
-    for sources in CALLS:
-        count = len(sources)
-        held = [] if ready is None else [own_result]
-        out = [
-            pl.pallas_call(
-                functools.partial(go_on, sources, ready),
-                out_shape=jax.ShapeDtypeStruct((4, assets, assets), jnp.bfloat16),
-                in_specs=[vmem] * (4 + count + len(held)) + [anywhere] * len(out),
-                out_specs=anywhere,
-                scratch_shapes=[
-                    pltpu.VMEM((count, 4, assets, 256), jnp.bfloat16),
-                    pltpu.SemaphoreType.DMA((count + len(held), 4, assets // CHUNK)),
-                ],
-                input_output_aliases={4 + count: 0} if out else {},
-                cost_estimate=pl.CostEstimate(
-                    flops=2_000_000_000 * count, bytes_accessed=2_000_000 * count, transcendentals=0
-                ),
-                compiler_params=PARAMS,
-                name="go_on",
-            )(mask, *prepared, *[quarters[source] for source in sources], *held, *out)
-        ]
-        ready = None
+    quarter = jax.ShapeDtypeStruct((4, assets, 256), jnp.bfloat16)
+    whole = jax.ShapeDtypeStruct((4, assets, assets), jnp.bfloat16)
+    out, ready, held = [], "own", own_result
+    for number, sources in enumerate(CALLS):
+        count, last = len(sources), number + 1 == len(CALLS)
+        out = pl.pallas_call(
+            functools.partial(go_on, sources, ready, None if last else sources[-1]),
+            out_shape=(whole,) if last else (whole, quarter),
+            in_specs=[vmem] * (5 + count) + [anywhere] * len(out),
+            out_specs=(anywhere,) if last else (anywhere, vmem),
+            scratch_shapes=[
+                pltpu.VMEM((count, 4, assets, 256), jnp.bfloat16),
+                pltpu.SemaphoreType.DMA((count + 1, 4, assets // CHUNK)),
+            ],
+            input_output_aliases={5 + count: 0} if out else {},
+            cost_estimate=pl.CostEstimate(
+                flops=2_000_000_000 * count, bytes_accessed=2_000_000 * count, transcendentals=0
+            ),
+            compiler_params=PARAMS,
+            name="go_on",
+        )(mask, *prepared, *[quarters[source] for source in sources], held, *out)
+        ready, out, held = sources[-1], out[:1], out[-1]
     return out[0]
 
 

time: 37.3 us -> 36.9 us (0.989)
  starting transfers between devices: 24.5 us -> 19.9 us
  waiting for transfers between devices: 2.5 us -> 6.38 us
  blocking collectives: 0 us -> 2.05 us
  other arithmetic: 0.8 us -> 0.03 us
  Pallas kernels: 7.79 us -> 7.06 us
    ppermute x3, waiting for transfers between devices: 0.01 us -> 5.31 us  [exchange_and_correlate(): quarters[source] = lax.ppermute(own, ('zh', 'zq'), links)]
    ppermute x3, starting transfers between devices: 8.48 us -> 3.94 us  [exchange_and_correlate(): quarters[source] = lax.ppermute(own, ('zh', 'zq'), links)]
    all_gather x0 -> x1, blocking collectives: none -> 2.05 us  [exchange_and_correlate(): pair = lax.all_gather(returns, 'c', axis=0)]
    ppermute x1 -> x0, waiting for transfers between devices: 1.42 us -> none  [exchange_and_correlate(): pair = jnp.stack([returns, lax.ppermute(returns, 'c', ring(2, 1))])]
    another operation x2 -> x1, other arithmetic: 0.79 us -> 0.02 us  [exchange_and_correlate(): own_rows = jnp.stack([pair, lax.ppermute(pair, 'yl', ring(2, 1))])]
    pallas_call x2, Pallas kernels: 5.28 us -> 4.54 us  [exchange_and_correlate(): pl.pallas_call(functools.partial(go_on, sources, ready, None if last else...]
  transfers between devices with their start and end apart: 10 -> 9, of which waited for: 2 -> 3; matrix products, arithmetic and copies ran while one was open for 0% -> 0% of each run, Pallas kernels for 13% -> 11%
where the time goes in v4:
time: 36.9 us; the launch traced here: 36.8 us
  starting transfers between devices  19.9 us (54%)
  Pallas kernels  7.06 us (19%)
  waiting for transfers between devices  6.38 us (17%)
  blocking collectives  2.05 us (6%)
  between operations  0.72 us (2%)
  local copies, waits for them, and re-layouts  0.65 us (2%)
    ppermute x1, starting transfers between devices, exchange_and_correlate(): turned = lax.ppermute(pair, AXES, corner_turn())  6.24 us
    ppermute x3, waiting for transfers between devices, exchange_and_correlate(): quarters[source] = lax.ppermute(own, ('zh', 'zq'), links)  5.31 us
    pallas_call x2, Pallas kernels, exchange_and_correlate(): pl.pallas_call(functools.partial(go_on, sources, ready, None if last else...  4.54 us
    ppermute x1, starting transfers between devices, exchange_and_correlate(): other = lax.ppermute(turned, 'yh', ring(2, 1))  4.47 us
    ppermute x3, starting transfers between devices, exchange_and_correlate(): quarters[source] = lax.ppermute(own, ('zh', 'zq'), links)  3.94 us
    ppermute x3, starting transfers between devices, exchange_and_correlate(): rows.append(lax.ppermute(own_rows, 'x', links))  3.56 us
    all_gather x1, blocking collectives, exchange_and_correlate(): pair = lax.all_gather(returns, 'c', axis=0)  2.05 us
    pallas_call x1, Pallas kernels, exchange_and_correlate(): pl.pallas_call(begin, out_shape=(jax.ShapeDtypeStruct((4, assets, LANES),...  1.96 us
  transfers between devices with their start and end apart: 9, of which 3 were waited for; matrix products, arithmetic and copies ran while one was open for 0% of the time, Pallas kernels for 11%

profile of v4, /device:TPU:4, one launch (start us, length us, event | category | flops | bytes accessed | tf_op | source)
XLA Modules:
  0.0 36.8 jit_solution(2811357163207678400)
XLA Ops:
  0.0 2.1 %all-gather = bf16[272,128]{1,0:T(8,128)(2,1)S(1)} all-gather(bf16[136,128]{1,0:T(8,128)(2,1)} %param.3), channel_id=2, replica_groups=mesh['yl'=2,'yh'=2,'zh'=2,'zq'=4,'x'=4,'c'=2] {'c'}, dimensions={0}, use_global_device_ids=true | all-gather | bytes 104448 | tf_op jit(solution)/shard_map/all_gather | solution.py:227
  2.1 1.6 %collective-permute-start = (bf16[2,136,128]{2,1,0:T(8,128)(2,1)S(1)}, bf16[2,136,128]{2,1,0:T(8,128)(2,1)S(1)}, u32[]{:S(2)}, u32[]{:S(2)}) collective-permute-start(bf16[2,136,128]{2,1,0:T(8,128)(2,1)S(1)} %bitcast.5), channel_id=1, source_target_pairs={{0,128},{128,0},{1,129},{129,1},{2,130},{130,2},{3,131},{131,3},{4... | collective-permute-start | bytes 208904 | tf_op jit(solution)/shard_map/ppermute | solution.py:229
  3.7 6.2 %collective-permute-start.4 = (bf16[2,136,128]{2,1,0:T(8,128)(2,1)S(1)}, bf16[2,136,128]{2,1,0:T(8,128)(2,1)S(1)}, u32[]{:S(2)}, u32[]{:S(2)}) collective-permute-start(bf16[2,136,128]{2,1,0:T(8,128)(2,1)S(1)} %bitcast.6), channel_id=1, source_target_pairs={{0,32},{1,0},{2,40},{3,8},{4,48},{5,16},{6,56},{7,24},{8,232},{9,2... | collective-permute-start | bytes 208904 | tf_op jit(solution)/shard_map/ppermute | solution.py:228
  10.6 0.0 collective-permute-done
  10.6 1.5 %collective-permute-start.3 = (bf16[2,2,136,128]{3,2,1,0:T(8,128)(2,1)S(1)}, bf16[2,2,136,128]{3,2,1,0:T(8,128)(2,1)S(1)}, u32[]{:S(2)}, u32[]{:S(2)}) collective-permute-start(bf16[2,2,136,128]{3,2,1,0:T(8,128)(2,1)S(1)} %pad_maximum_fusion.own), channel_id=1, source_target_pairs={{0,4},{2,6},{4,0},{6,2},{1,5},{3,7},{5,1},{7,3},{8,12},{10,14},{12... | collective-permute-start | bytes 417800 | tf_op jit(solution)/shard_map/ppermute | solution.py:233
  12.2 0.7 %collective-permute-start.2 = (bf16[2,2,136,128]{3,2,1,0:T(8,128)(2,1)S(1)}, bf16[2,2,136,128]{3,2,1,0:T(8,128)(2,1)S(1)}, u32[]{:S(2)}, u32[]{:S(2)}) collective-permute-start(bf16[2,2,136,128]{3,2,1,0:T(8,128)(2,1)S(1)} %pad_maximum_fusion.own), channel_id=1, source_target_pairs={{0,6},{2,0},{4,2},{6,4},{1,7},{3,1},{5,3},{7,5},{8,14},{10,8},{12,... | collective-permute-start | bytes 417800 | tf_op jit(solution)/shard_map/ppermute | solution.py:233
  12.9 1.3 %collective-permute-start.1 = (bf16[2,2,136,128]{3,2,1,0:T(8,128)(2,1)S(1)}, bf16[2,2,136,128]{3,2,1,0:T(8,128)(2,1)S(1)}, u32[]{:S(2)}, u32[]{:S(2)}) collective-permute-start(bf16[2,2,136,128]{3,2,1,0:T(8,128)(2,1)S(1)} %pad_maximum_fusion.own), channel_id=1, source_target_pairs={{0,2},{2,4},{4,6},{6,0},{1,3},{3,5},{5,7},{7,1},{8,10},{10,12},{12... | collective-permute-start | bytes 417800 | tf_op jit(solution)/shard_map/ppermute | solution.py:233
  14.2 0.0 collective-permute-done.4
  14.2 4.5 %collective-permute-start.5 = (bf16[2,136,128]{2,1,0:T(8,128)(2,1)S(1)}, bf16[2,136,128]{2,1,0:T(8,128)(2,1)S(1)}, u32[]{:S(2)}, u32[]{:S(2)}) collective-permute-start(bf16[2,136,128]{2,1,0:T(8,128)(2,1)S(1)} %collective-permute-done.4), channel_id=1, source_target_pairs={{0,64},{64,0},{1,65},{65,1},{2,66},{66,2},{3,67},{67,3},{4,68},{68... | collective-permute-start | bytes 208904 | tf_op jit(solution)/shard_map/ppermute | solution.py:230
  18.7 0.7 %copy-done = s32[4]{0:T(128)S(1)} copy-done((s32[4]{0:T(128)S(1)}, s32[4]{0:T(128)}, u32[]{:S(2)}) %copy-start) | copy-done | bytes 40
  19.3 0.6 %write_masks.1.mask = f32[368,128]{1,0:T(8,128)S(1)} custom-call(s32[1]{0:T(128)S(6)} %copy.6.window, s32[4]{0:T(128)S(1)} %copy-done), custom_call_target="tpu_custom_call" | custom-call | flops 1000000000 | bytes 200000 | tf_op jit(solution)/shard_map/write_masks/pallas_call | solution.py:218
  19.9 1.1 %collective-permute-done.5 = bf16[2,136,128]{2,1,0:T(8,128)(2,1)S(1)} collective-permute-done((bf16[2,136,128]{2,1,0:T(8,128)(2,1)S(1)}, bf16[2,136,128]{2,1,0:T(8,128)(2,1)S(1)}, u32[]{:S(2)}, u32[]{:S(2)}) %collective-permute-start.5) | collective-permute-done | bytes 69664 | tf_op jit(solution)/shard_map/ppermute | solution.py:230
  21.0 1.8 %collective-permute-start.8 = (bf16[2,2,136,128]{3,2,1,0:T(8,128)(2,1)S(1)}, bf16[2,2,136,128]{3,2,1,0:T(8,128)(2,1)S(1)}, u32[]{:S(2)}, u32[]{:S(2)}) collective-permute-start(bf16[2,2,136,128]{3,2,1,0:T(8,128)(2,1)S(1)} %pad_maximum_fusion.1.own_block), channel_id=1, source_target_pairs={{0,8},{8,16},{16,24},{24,32},{32,40},{40,48},{48,56},{56,0},{1,9},... | collective-permute-start | bytes 417800 | tf_op jit(solution)/shard_map/ppermute | solution.py:237
  22.7 2.2 %collective-permute-start.7 = (bf16[2,2,136,128]{3,2,1,0:T(8,128)(2,1)S(1)}, bf16[2,2,136,128]{3,2,1,0:T(8,128)(2,1)S(1)}, u32[]{:S(2)}, u32[]{:S(2)}) collective-permute-start(bf16[2,2,136,128]{3,2,1,0:T(8,128)(2,1)S(1)} %pad_maximum_fusion.1.own_block), channel_id=1, source_target_pairs={{0,56},{8,0},{16,8},{24,16},{32,24},{40,32},{48,40},{56,48},{1,57}... | collective-permute-start | bytes 417800 | tf_op jit(solution)/shard_map/ppermute | solution.py:237
  24.9 0.0 collective-permute-done.3.across
  24.9 0.0 collective-permute-start.6
  24.9 0.0 collective-permute-done.2.after
  24.9 0.0 collective-permute-done.1.before
  24.9 2.0 %begin.1 = (bf16[4,1024,128]{2,1,0:T(8,128)(2,1)S(1)}, bf16[1024,128]{1,0:T(8,128)(2,1)S(1)}, f32[8,1024,128]{2,1,0:T(8,128)S(1)}, bf16[4,1024,256]{2,1,0:T(8,128)(2,1)S(1)}) custom-call(f32[368,128]{1,0:T(8,128)S(1)} %write_masks.1.mask, bf16[2,2,136,128]{3,2,1,0:T(8,128)(2,1)S(1)} %pad_maximum_fusion.own, ...), custom_call_target="tpu_custom_call" | custom-call | flops 4000000000 | bytes 4000000 | tf_op jit(solution)/shard_map/begin/pallas_call | solution.py:239
  26.9 1.9 %collective-permute-done.8.refs_0_ = bf16[2,2,136,128]{3,2,1,0:T(8,128)(2,1)S(1)} collective-permute-done((bf16[2,2,136,128]{3,2,1,0:T(8,128)(2,1)S(1)}, bf16[2,2,136,128]{3,2,1,0:T(8,128)(2,1)S(1)}, u32[]{:S(2)}, u32[]{:S(2)}) %collective-permute-start.8) | collective-permute-done | bytes 139296 | tf_op jit(solution)/shard_map/ppermute | solution.py:237
  28.8 1.4 %go_on.2 = (bf16[4,1024,1024]{2,1,0:T(8,128)(2,1)}, bf16[4,1024,256]{2,1,0:T(8,128)(2,1)S(1)}) custom-call(f32[368,128]{1,0:T(8,128)S(1)} %write_masks.1.mask, bf16[4,1024,128]{2,1,0:T(8,128)(2,1)S(1)} %get-tuple-element.11.low, bf16[1024,128]{1,0:T(8,128)(2,1)S(1)} %get-tuple-element.12.high, f32[8,1024,128]{2,1,0:T(8,128)S(1)} %get-tuple-element.13.spread, ...), custom_call_target="tpu_custom_call" | custom-call | flops 2000000000 | bytes 2000000 | tf_op jit(solution)/shard_map/go_on/pallas_call | solution.py:258
  30.2 0.0 collective-permute-done.7.refs_1_
  30.2 3.4 %collective-permute-done.6.refs_0_ = bf16[2,2,136,128]{3,2,1,0:T(8,128)(2,1)S(1)} collective-permute-done((bf16[2,2,136,128]{3,2,1,0:T(8,128)(2,1)S(1)}, bf16[2,2,136,128]{3,2,1,0:T(8,128)(2,1)S(1)}, u32[]{:S(2)}, u32[]{:S(2)}) %collective-permute-start.6) | collective-permute-done | bytes 139296 | tf_op jit(solution)/shard_map/ppermute | solution.py:237
  33.7 3.1 %go_on.3 = bf16[4,1024,1024]{2,1,0:T(8,128)(2,1)} custom-call(f32[368,128]{1,0:T(8,128)S(1)} %write_masks.1.mask, bf16[4,1024,128]{2,1,0:T(8,128)(2,1)S(1)} %get-tuple-element.11.low, bf16[1024,128]{1,0:T(8,128)(2,1)S(1)} %get-tuple-element.12.high, f32[8,1024,128]{2,1,0:T(8,128)S(1)} %get-tuple-element.13.spread, ...), custom_call_target="tpu_custom_call", output_to_operand_aliasing={{}: (7, {})} | custom-call | flops 4000000000 | bytes 4000000 | tf_op jit(solution)/shard_map/go_on/pallas_call | solution.py:258
  (3 shorter events, 0.0 us)
Async XLA Ops:
  2.1 8.5 %collective-permute-start = (bf16[2,136,128]{2,1,0:T(8,128)(2,1)S(1)}, bf16[2,136,128]{2,1,0:T(8,128)(2,1)S(1)}, u32[]{:S(2)}, u32[]{:S(2)}) collective-permute-start(bf16[2,136,128]{2,1,0:T(8,128)(2,1)S(1)} %bitcast.5), channel_id=1, source_target_pairs={{0,128},{128,0},{1,129},{129,1},{2,130},{130,2},{3,131},{131,3},{4... | collective-permute-start | bytes 208904 | tf_op jit(solution)/shard_map/ppermute | solution.py:229
  3.7 10.5 %collective-permute-start.4 = (bf16[2,136,128]{2,1,0:T(8,128)(2,1)S(1)}, bf16[2,136,128]{2,1,0:T(8,128)(2,1)S(1)}, u32[]{:S(2)}, u32[]{:S(2)}) collective-permute-start(bf16[2,136,128]{2,1,0:T(8,128)(2,1)S(1)} %bitcast.6), channel_id=1, source_target_pairs={{0,32},{1,0},{2,40},{3,8},{4,48},{5,16},{6,56},{7,24},{8,232},{9,2... | collective-permute-start | bytes 208904 | tf_op jit(solution)/shard_map/ppermute | solution.py:228
  10.6 14.3 %collective-permute-start.3 = (bf16[2,2,136,128]{3,2,1,0:T(8,128)(2,1)S(1)}, bf16[2,2,136,128]{3,2,1,0:T(8,128)(2,1)S(1)}, u32[]{:S(2)}, u32[]{:S(2)}) collective-permute-start(bf16[2,2,136,128]{3,2,1,0:T(8,128)(2,1)S(1)} %pad_maximum_fusion.own), channel_id=1, source_target_pairs={{0,4},{2,6},{4,0},{6,2},{1,5},{3,7},{5,1},{7,3},{8,12},{10,14},{12... | collective-permute-start | bytes 417800 | tf_op jit(solution)/shard_map/ppermute | solution.py:233
  12.2 12.8 %collective-permute-start.2 = (bf16[2,2,136,128]{3,2,1,0:T(8,128)(2,1)S(1)}, bf16[2,2,136,128]{3,2,1,0:T(8,128)(2,1)S(1)}, u32[]{:S(2)}, u32[]{:S(2)}) collective-permute-start(bf16[2,2,136,128]{3,2,1,0:T(8,128)(2,1)S(1)} %pad_maximum_fusion.own), channel_id=1, source_target_pairs={{0,6},{2,0},{4,2},{6,4},{1,7},{3,1},{5,3},{7,5},{8,14},{10,8},{12,... | collective-permute-start | bytes 417800 | tf_op jit(solution)/shard_map/ppermute | solution.py:233
  12.9 12.0 %collective-permute-start.1 = (bf16[2,2,136,128]{3,2,1,0:T(8,128)(2,1)S(1)}, bf16[2,2,136,128]{3,2,1,0:T(8,128)(2,1)S(1)}, u32[]{:S(2)}, u32[]{:S(2)}) collective-permute-start(bf16[2,2,136,128]{3,2,1,0:T(8,128)(2,1)S(1)} %pad_maximum_fusion.own), channel_id=1, source_target_pairs={{0,2},{2,4},{4,6},{6,0},{1,3},{3,5},{5,7},{7,1},{8,10},{10,12},{12... | collective-permute-start | bytes 417800 | tf_op jit(solution)/shard_map/ppermute | solution.py:233
  14.2 6.8 %collective-permute-start.5 = (bf16[2,136,128]{2,1,0:T(8,128)(2,1)S(1)}, bf16[2,136,128]{2,1,0:T(8,128)(2,1)S(1)}, u32[]{:S(2)}, u32[]{:S(2)}) collective-permute-start(bf16[2,136,128]{2,1,0:T(8,128)(2,1)S(1)} %collective-permute-done.4), channel_id=1, source_target_pairs={{0,64},{64,0},{1,65},{65,1},{2,66},{66,2},{3,67},{67,3},{4,68},{68... | collective-permute-start | bytes 208904 | tf_op jit(solution)/shard_map/ppermute | solution.py:230
  18.7 0.7 %copy-start = (s32[4]{0:T(128)S(1)}, s32[4]{0:T(128)}, u32[]{:S(2)}) copy-start(s32[4]{0:T(128)} %out_days.1) | copy-start | bytes 52
  21.0 7.8 %collective-permute-start.8 = (bf16[2,2,136,128]{3,2,1,0:T(8,128)(2,1)S(1)}, bf16[2,2,136,128]{3,2,1,0:T(8,128)(2,1)S(1)}, u32[]{:S(2)}, u32[]{:S(2)}) collective-permute-start(bf16[2,2,136,128]{3,2,1,0:T(8,128)(2,1)S(1)} %pad_maximum_fusion.1.own_block), channel_id=1, source_target_pairs={{0,8},{8,16},{16,24},{24,32},{32,40},{40,48},{48,56},{56,0},{1,9},... | collective-permute-start | bytes 417800 | tf_op jit(solution)/shard_map/ppermute | solution.py:237
  22.7 7.5 %collective-permute-start.7 = (bf16[2,2,136,128]{3,2,1,0:T(8,128)(2,1)S(1)}, bf16[2,2,136,128]{3,2,1,0:T(8,128)(2,1)S(1)}, u32[]{:S(2)}, u32[]{:S(2)}) collective-permute-start(bf16[2,2,136,128]{3,2,1,0:T(8,128)(2,1)S(1)} %pad_maximum_fusion.1.own_block), channel_id=1, source_target_pairs={{0,56},{8,0},{16,8},{24,16},{32,24},{40,32},{48,40},{56,48},{1,57}... | collective-permute-start | bytes 417800 | tf_op jit(solution)/shard_map/ppermute | solution.py:237
  24.9 8.8 %collective-permute-start.6 = (bf16[2,2,136,128]{3,2,1,0:T(8,128)(2,1)S(1)}, bf16[2,2,136,128]{3,2,1,0:T(8,128)(2,1)S(1)}, u32[]{:S(2)}, u32[]{:S(2)}) collective-permute-start(bf16[2,2,136,128]{3,2,1,0:T(8,128)(2,1)S(1)} %pad_maximum_fusion.1.own_block), channel_id=1, source_target_pairs={{0,16},{8,56},{16,32},{24,8},{32,48},{40,24},{48,0},{56,40},{1,17}... | collective-permute-start | bytes 417800 | tf_op jit(solution)/shard_map/ppermute | solution.py:237

commit v5 on v4

--- a/solution.py
+++ b/solution.py
@@ -18,7 +18,8 @@
 CHUNK = 512
 ORDER = ("before", "across", "after")
 CALLS = (ORDER[:1], ORDER[1:])
-PARAMS = pltpu.CompilerParams(vmem_limit_bytes=24 * 2**20)
+GRANT = 24 * 2**20
+PARAMS = pltpu.CompilerParams(vmem_limit_bytes=GRANT)
 
 
 def place(yl, yh, zh, zq, x, c):
@@ -268,7 +269,7 @@
             cost_estimate=pl.CostEstimate(
                 flops=2_000_000_000 * count, bytes_accessed=2_000_000 * count, transcendentals=0
             ),
-            compiler_params=PARAMS,
+            compiler_params=pltpu.CompilerParams(vmem_limit_bytes=GRANT),
             name="go_on",
         )(mask, *prepared, *[quarters[source] for source in sources], held, *out)
         ready, out, held = sources[-1], out[:1], out[-1]

time: 36.9 us -> 36.9 us (level)
  no operation moved by 1% of the time
where the time goes in v5:
time: 36.9 us; the launch traced here: 36.8 us
  starting transfers between devices  19.9 us (54%)
  Pallas kernels  7.06 us (19%)
  waiting for transfers between devices  6.38 us (17%)
  blocking collectives  2.05 us (6%)
  between operations  0.72 us (2%)
  local copies, waits for them, and re-layouts  0.65 us (2%)
    ppermute x1, starting transfers between devices, exchange_and_correlate(): turned = lax.ppermute(pair, AXES, corner_turn())  6.24 us
    ppermute x3, waiting for transfers between devices, exchange_and_correlate(): quarters[source] = lax.ppermute(own, ('zh', 'zq'), links)  5.31 us
    pallas_call x2, Pallas kernels, exchange_and_correlate(): pl.pallas_call(functools.partial(go_on, sources, ready, None if last else...  4.54 us
    ppermute x1, starting transfers between devices, exchange_and_correlate(): other = lax.ppermute(turned, 'yh', ring(2, 1))  4.47 us
    ppermute x3, starting transfers between devices, exchange_and_correlate(): quarters[source] = lax.ppermute(own, ('zh', 'zq'), links)  3.94 us
    ppermute x3, starting transfers between devices, exchange_and_correlate(): rows.append(lax.ppermute(own_rows, 'x', links))  3.56 us
    all_gather x1, blocking collectives, exchange_and_correlate(): pair = lax.all_gather(returns, 'c', axis=0)  2.05 us
    pallas_call x1, Pallas kernels, exchange_and_correlate(): pl.pallas_call(begin, out_shape=(jax.ShapeDtypeStruct((4, assets, LANES),...  1.96 us
  transfers between devices with their start and end apart: 9, of which 3 were waited for; matrix products, arithmetic and copies ran while one was open for 0% of the time, Pallas kernels for 11%

profile of v5, /device:TPU:4, one launch (start us, length us, event | category | flops | bytes accessed | tf_op | source)
XLA Modules:
  0.0 36.8 jit_solution(2811357163207678400)
XLA Ops:
  0.0 2.1 %all-gather = bf16[272,128]{1,0:T(8,128)(2,1)S(1)} all-gather(bf16[136,128]{1,0:T(8,128)(2,1)} %param.3), channel_id=2, replica_groups=mesh['yl'=2,'yh'=2,'zh'=2,'zq'=4,'x'=4,'c'=2] {'c'}, dimensions={0}, use_global_device_ids=true | all-gather | bytes 104448 | tf_op jit(solution)/shard_map/all_gather | solution.py:228
  2.1 1.6 %collective-permute-start = (bf16[2,136,128]{2,1,0:T(8,128)(2,1)S(1)}, bf16[2,136,128]{2,1,0:T(8,128)(2,1)S(1)}, u32[]{:S(2)}, u32[]{:S(2)}) collective-permute-start(bf16[2,136,128]{2,1,0:T(8,128)(2,1)S(1)} %bitcast.5), channel_id=1, source_target_pairs={{0,128},{128,0},{1,129},{129,1},{2,130},{130,2},{3,131},{131,3},{4... | collective-permute-start | bytes 208904 | tf_op jit(solution)/shard_map/ppermute | solution.py:230
  3.7 6.2 %collective-permute-start.4 = (bf16[2,136,128]{2,1,0:T(8,128)(2,1)S(1)}, bf16[2,136,128]{2,1,0:T(8,128)(2,1)S(1)}, u32[]{:S(2)}, u32[]{:S(2)}) collective-permute-start(bf16[2,136,128]{2,1,0:T(8,128)(2,1)S(1)} %bitcast.6), channel_id=1, source_target_pairs={{0,32},{1,0},{2,40},{3,8},{4,48},{5,16},{6,56},{7,24},{8,232},{9,2... | collective-permute-start | bytes 208904 | tf_op jit(solution)/shard_map/ppermute | solution.py:229
  10.6 0.0 collective-permute-done
  10.6 1.5 %collective-permute-start.3 = (bf16[2,2,136,128]{3,2,1,0:T(8,128)(2,1)S(1)}, bf16[2,2,136,128]{3,2,1,0:T(8,128)(2,1)S(1)}, u32[]{:S(2)}, u32[]{:S(2)}) collective-permute-start(bf16[2,2,136,128]{3,2,1,0:T(8,128)(2,1)S(1)} %pad_maximum_fusion.own), channel_id=1, source_target_pairs={{0,4},{2,6},{4,0},{6,2},{1,5},{3,7},{5,1},{7,3},{8,12},{10,14},{12... | collective-permute-start | bytes 417800 | tf_op jit(solution)/shard_map/ppermute | solution.py:234
  12.2 0.7 %collective-permute-start.2 = (bf16[2,2,136,128]{3,2,1,0:T(8,128)(2,1)S(1)}, bf16[2,2,136,128]{3,2,1,0:T(8,128)(2,1)S(1)}, u32[]{:S(2)}, u32[]{:S(2)}) collective-permute-start(bf16[2,2,136,128]{3,2,1,0:T(8,128)(2,1)S(1)} %pad_maximum_fusion.own), channel_id=1, source_target_pairs={{0,6},{2,0},{4,2},{6,4},{1,7},{3,1},{5,3},{7,5},{8,14},{10,8},{12,... | collective-permute-start | bytes 417800 | tf_op jit(solution)/shard_map/ppermute | solution.py:234
  12.9 1.3 %collective-permute-start.1 = (bf16[2,2,136,128]{3,2,1,0:T(8,128)(2,1)S(1)}, bf16[2,2,136,128]{3,2,1,0:T(8,128)(2,1)S(1)}, u32[]{:S(2)}, u32[]{:S(2)}) collective-permute-start(bf16[2,2,136,128]{3,2,1,0:T(8,128)(2,1)S(1)} %pad_maximum_fusion.own), channel_id=1, source_target_pairs={{0,2},{2,4},{4,6},{6,0},{1,3},{3,5},{5,7},{7,1},{8,10},{10,12},{12... | collective-permute-start | bytes 417800 | tf_op jit(solution)/shard_map/ppermute | solution.py:234
  14.2 0.0 collective-permute-done.4
  14.2 4.5 %collective-permute-start.5 = (bf16[2,136,128]{2,1,0:T(8,128)(2,1)S(1)}, bf16[2,136,128]{2,1,0:T(8,128)(2,1)S(1)}, u32[]{:S(2)}, u32[]{:S(2)}) collective-permute-start(bf16[2,136,128]{2,1,0:T(8,128)(2,1)S(1)} %collective-permute-done.4), channel_id=1, source_target_pairs={{0,64},{64,0},{1,65},{65,1},{2,66},{66,2},{3,67},{67,3},{4,68},{68... | collective-permute-start | bytes 208904 | tf_op jit(solution)/shard_map/ppermute | solution.py:231
  18.7 0.7 %copy-done = s32[4]{0:T(128)S(1)} copy-done((s32[4]{0:T(128)S(1)}, s32[4]{0:T(128)}, u32[]{:S(2)}) %copy-start) | copy-done | bytes 40
  19.3 0.6 %write_masks.1.mask = f32[368,128]{1,0:T(8,128)S(1)} custom-call(s32[1]{0:T(128)S(6)} %copy.6.window, s32[4]{0:T(128)S(1)} %copy-done), custom_call_target="tpu_custom_call" | custom-call | flops 1000000000 | bytes 200000 | tf_op jit(solution)/shard_map/write_masks/pallas_call | solution.py:219
  19.9 1.1 %collective-permute-done.5 = bf16[2,136,128]{2,1,0:T(8,128)(2,1)S(1)} collective-permute-done((bf16[2,136,128]{2,1,0:T(8,128)(2,1)S(1)}, bf16[2,136,128]{2,1,0:T(8,128)(2,1)S(1)}, u32[]{:S(2)}, u32[]{:S(2)}) %collective-permute-start.5) | collective-permute-done | bytes 69664 | tf_op jit(solution)/shard_map/ppermute | solution.py:231
  21.0 1.8 %collective-permute-start.8 = (bf16[2,2,136,128]{3,2,1,0:T(8,128)(2,1)S(1)}, bf16[2,2,136,128]{3,2,1,0:T(8,128)(2,1)S(1)}, u32[]{:S(2)}, u32[]{:S(2)}) collective-permute-start(bf16[2,2,136,128]{3,2,1,0:T(8,128)(2,1)S(1)} %pad_maximum_fusion.1.own_block), channel_id=1, source_target_pairs={{0,8},{8,16},{16,24},{24,32},{32,40},{40,48},{48,56},{56,0},{1,9},... | collective-permute-start | bytes 417800 | tf_op jit(solution)/shard_map/ppermute | solution.py:238
  22.7 2.2 %collective-permute-start.7 = (bf16[2,2,136,128]{3,2,1,0:T(8,128)(2,1)S(1)}, bf16[2,2,136,128]{3,2,1,0:T(8,128)(2,1)S(1)}, u32[]{:S(2)}, u32[]{:S(2)}) collective-permute-start(bf16[2,2,136,128]{3,2,1,0:T(8,128)(2,1)S(1)} %pad_maximum_fusion.1.own_block), channel_id=1, source_target_pairs={{0,56},{8,0},{16,8},{24,16},{32,24},{40,32},{48,40},{56,48},{1,57}... | collective-permute-start | bytes 417800 | tf_op jit(solution)/shard_map/ppermute | solution.py:238
  24.9 0.0 collective-permute-done.3.across
  24.9 0.0 collective-permute-start.6
  24.9 0.0 collective-permute-done.2.after
  24.9 0.0 collective-permute-done.1.before
  24.9 2.0 %begin.1 = (bf16[4,1024,128]{2,1,0:T(8,128)(2,1)S(1)}, bf16[1024,128]{1,0:T(8,128)(2,1)S(1)}, f32[8,1024,128]{2,1,0:T(8,128)S(1)}, bf16[4,1024,256]{2,1,0:T(8,128)(2,1)S(1)}) custom-call(f32[368,128]{1,0:T(8,128)S(1)} %write_masks.1.mask, bf16[2,2,136,128]{3,2,1,0:T(8,128)(2,1)S(1)} %pad_maximum_fusion.own, ...), custom_call_target="tpu_custom_call" | custom-call | flops 4000000000 | bytes 4000000 | tf_op jit(solution)/shard_map/begin/pallas_call | solution.py:240
  26.9 1.9 %collective-permute-done.8.refs_0_ = bf16[2,2,136,128]{3,2,1,0:T(8,128)(2,1)S(1)} collective-permute-done((bf16[2,2,136,128]{3,2,1,0:T(8,128)(2,1)S(1)}, bf16[2,2,136,128]{3,2,1,0:T(8,128)(2,1)S(1)}, u32[]{:S(2)}, u32[]{:S(2)}) %collective-permute-start.8) | collective-permute-done | bytes 139296 | tf_op jit(solution)/shard_map/ppermute | solution.py:238
  28.8 1.4 %go_on.2 = (bf16[4,1024,1024]{2,1,0:T(8,128)(2,1)}, bf16[4,1024,256]{2,1,0:T(8,128)(2,1)S(1)}) custom-call(f32[368,128]{1,0:T(8,128)S(1)} %write_masks.1.mask, bf16[4,1024,128]{2,1,0:T(8,128)(2,1)S(1)} %get-tuple-element.11.low, bf16[1024,128]{1,0:T(8,128)(2,1)S(1)} %get-tuple-element.12.high, f32[8,1024,128]{2,1,0:T(8,128)S(1)} %get-tuple-element.13.spread, ...), custom_call_target="tpu_custom_call" | custom-call | flops 2000000000 | bytes 2000000 | tf_op jit(solution)/shard_map/go_on/pallas_call | solution.py:259
  30.2 0.0 collective-permute-done.7.refs_1_
  30.2 3.4 %collective-permute-done.6.refs_0_ = bf16[2,2,136,128]{3,2,1,0:T(8,128)(2,1)S(1)} collective-permute-done((bf16[2,2,136,128]{3,2,1,0:T(8,128)(2,1)S(1)}, bf16[2,2,136,128]{3,2,1,0:T(8,128)(2,1)S(1)}, u32[]{:S(2)}, u32[]{:S(2)}) %collective-permute-start.6) | collective-permute-done | bytes 139296 | tf_op jit(solution)/shard_map/ppermute | solution.py:238
  33.7 3.1 %go_on.3 = bf16[4,1024,1024]{2,1,0:T(8,128)(2,1)} custom-call(f32[368,128]{1,0:T(8,128)S(1)} %write_masks.1.mask, bf16[4,1024,128]{2,1,0:T(8,128)(2,1)S(1)} %get-tuple-element.11.low, bf16[1024,128]{1,0:T(8,128)(2,1)S(1)} %get-tuple-element.12.high, f32[8,1024,128]{2,1,0:T(8,128)S(1)} %get-tuple-element.13.spread, ...), custom_call_target="tpu_custom_call", output_to_operand_aliasing={{}: (7, {})} | custom-call | flops 4000000000 | bytes 4000000 | tf_op jit(solution)/shard_map/go_on/pallas_call | solution.py:259
  (3 shorter events, 0.0 us)
Async XLA Ops:
  2.1 8.5 %collective-permute-start = (bf16[2,136,128]{2,1,0:T(8,128)(2,1)S(1)}, bf16[2,136,128]{2,1,0:T(8,128)(2,1)S(1)}, u32[]{:S(2)}, u32[]{:S(2)}) collective-permute-start(bf16[2,136,128]{2,1,0:T(8,128)(2,1)S(1)} %bitcast.5), channel_id=1, source_target_pairs={{0,128},{128,0},{1,129},{129,1},{2,130},{130,2},{3,131},{131,3},{4... | collective-permute-start | bytes 208904 | tf_op jit(solution)/shard_map/ppermute | solution.py:230
  3.7 10.5 %collective-permute-start.4 = (bf16[2,136,128]{2,1,0:T(8,128)(2,1)S(1)}, bf16[2,136,128]{2,1,0:T(8,128)(2,1)S(1)}, u32[]{:S(2)}, u32[]{:S(2)}) collective-permute-start(bf16[2,136,128]{2,1,0:T(8,128)(2,1)S(1)} %bitcast.6), channel_id=1, source_target_pairs={{0,32},{1,0},{2,40},{3,8},{4,48},{5,16},{6,56},{7,24},{8,232},{9,2... | collective-permute-start | bytes 208904 | tf_op jit(solution)/shard_map/ppermute | solution.py:229
  10.6 14.3 %collective-permute-start.3 = (bf16[2,2,136,128]{3,2,1,0:T(8,128)(2,1)S(1)}, bf16[2,2,136,128]{3,2,1,0:T(8,128)(2,1)S(1)}, u32[]{:S(2)}, u32[]{:S(2)}) collective-permute-start(bf16[2,2,136,128]{3,2,1,0:T(8,128)(2,1)S(1)} %pad_maximum_fusion.own), channel_id=1, source_target_pairs={{0,4},{2,6},{4,0},{6,2},{1,5},{3,7},{5,1},{7,3},{8,12},{10,14},{12... | collective-permute-start | bytes 417800 | tf_op jit(solution)/shard_map/ppermute | solution.py:234
  12.2 12.8 %collective-permute-start.2 = (bf16[2,2,136,128]{3,2,1,0:T(8,128)(2,1)S(1)}, bf16[2,2,136,128]{3,2,1,0:T(8,128)(2,1)S(1)}, u32[]{:S(2)}, u32[]{:S(2)}) collective-permute-start(bf16[2,2,136,128]{3,2,1,0:T(8,128)(2,1)S(1)} %pad_maximum_fusion.own), channel_id=1, source_target_pairs={{0,6},{2,0},{4,2},{6,4},{1,7},{3,1},{5,3},{7,5},{8,14},{10,8},{12,... | collective-permute-start | bytes 417800 | tf_op jit(solution)/shard_map/ppermute | solution.py:234
  12.9 12.0 %collective-permute-start.1 = (bf16[2,2,136,128]{3,2,1,0:T(8,128)(2,1)S(1)}, bf16[2,2,136,128]{3,2,1,0:T(8,128)(2,1)S(1)}, u32[]{:S(2)}, u32[]{:S(2)}) collective-permute-start(bf16[2,2,136,128]{3,2,1,0:T(8,128)(2,1)S(1)} %pad_maximum_fusion.own), channel_id=1, source_target_pairs={{0,2},{2,4},{4,6},{6,0},{1,3},{3,5},{5,7},{7,1},{8,10},{10,12},{12... | collective-permute-start | bytes 417800 | tf_op jit(solution)/shard_map/ppermute | solution.py:234
  14.2 6.8 %collective-permute-start.5 = (bf16[2,136,128]{2,1,0:T(8,128)(2,1)S(1)}, bf16[2,136,128]{2,1,0:T(8,128)(2,1)S(1)}, u32[]{:S(2)}, u32[]{:S(2)}) collective-permute-start(bf16[2,136,128]{2,1,0:T(8,128)(2,1)S(1)} %collective-permute-done.4), channel_id=1, source_target_pairs={{0,64},{64,0},{1,65},{65,1},{2,66},{66,2},{3,67},{67,3},{4,68},{68... | collective-permute-start | bytes 208904 | tf_op jit(solution)/shard_map/ppermute | solution.py:231
  18.7 0.7 %copy-start = (s32[4]{0:T(128)S(1)}, s32[4]{0:T(128)}, u32[]{:S(2)}) copy-start(s32[4]{0:T(128)} %out_days.1) | copy-start | bytes 52
  21.0 7.8 %collective-permute-start.8 = (bf16[2,2,136,128]{3,2,1,0:T(8,128)(2,1)S(1)}, bf16[2,2,136,128]{3,2,1,0:T(8,128)(2,1)S(1)}, u32[]{:S(2)}, u32[]{:S(2)}) collective-permute-start(bf16[2,2,136,128]{3,2,1,0:T(8,128)(2,1)S(1)} %pad_maximum_fusion.1.own_block), channel_id=1, source_target_pairs={{0,8},{8,16},{16,24},{24,32},{32,40},{40,48},{48,56},{56,0},{1,9},... | collective-permute-start | bytes 417800 | tf_op jit(solution)/shard_map/ppermute | solution.py:238
  22.7 7.5 %collective-permute-start.7 = (bf16[2,2,136,128]{3,2,1,0:T(8,128)(2,1)S(1)}, bf16[2,2,136,128]{3,2,1,0:T(8,128)(2,1)S(1)}, u32[]{:S(2)}, u32[]{:S(2)}) collective-permute-start(bf16[2,2,136,128]{3,2,1,0:T(8,128)(2,1)S(1)} %pad_maximum_fusion.1.own_block), channel_id=1, source_target_pairs={{0,56},{8,0},{16,8},{24,16},{32,24},{40,32},{48,40},{56,48},{1,57}... | collective-permute-start | bytes 417800 | tf_op jit(solution)/shard_map/ppermute | solution.py:238
  24.9 8.8 %collective-permute-start.6 = (bf16[2,2,136,128]{3,2,1,0:T(8,128)(2,1)S(1)}, bf16[2,2,136,128]{3,2,1,0:T(8,128)(2,1)S(1)}, u32[]{:S(2)}, u32[]{:S(2)}) collective-permute-start(bf16[2,2,136,128]{3,2,1,0:T(8,128)(2,1)S(1)} %pad_maximum_fusion.1.own_block), channel_id=1, source_target_pairs={{0,16},{8,56},{16,32},{24,8},{32,48},{40,24},{48,0},{56,40},{1,17}... | collective-permute-start | bytes 417800 | tf_op jit(solution)/shard_map/ppermute | solution.py:238
